TPU v7x, 32 devices: a whole 2x2x4 slice. The times are simulated.
32 devices in a mesh: gx: 2 (over x), gy: 4 (over z), gz: 4 (over y, core).
Axes of the slice: x: 2, y: 2, z: 4, core: 2. Of those that a mesh axis runs over, the one named last changes fastest.
Arguments:
- right_side: float32 [128, 256, 1024], P('gx', 'gy', 'gz'), may hold values from -5 to 7
- initial_guess: float32 [128, 256, 1024], P('gx', 'gy', 'gz'), may hold values from -5 to 7
Outputs:
- solution: float32 [128, 256, 1024], P('gx', 'gy', 'gz')
All inputs are finite; a program needn't handle non-finite values.
Results may differ from a plain program's by a relative error of at most 0.000028.
Values sent between devices are 32-bit elements; how exact they have to be, the bound alone decides.
A program may use at most 128 MiB of HBM per device.

v0:
```python
import functools
import itertools

import jax
import jax.numpy as jnp
from jax import lax
from jax.experimental import pallas as pl
from jax.experimental.pallas import tpu as pltpu
from jax.sharding import PartitionSpec as P

COARSE_SWEEPS = 6
LANES = 128
AXES = ("gx", "gy", "gz")
relax_weight = 0.8


def dot_exact(a, w):
    hi = a.astype(jnp.bfloat16)
    rest = a - hi.astype(jnp.float32)
    mid = rest.astype(jnp.bfloat16)
    low = (rest - mid.astype(jnp.float32)).astype(jnp.bfloat16)
    dot = functools.partial(jnp.dot, preferred_element_type=jnp.float32)
    return dot(hi, w) + (dot(mid, w) + dot(low, w))


def iotas(shape):
    return (
        lax.broadcasted_iota(jnp.int32, shape, 0),
        lax.broadcasted_iota(jnp.int32, shape, 1),
    )


def restrict_matrix(rows, cols, count, wrap=None):
    r, c = iotas((rows, cols))
    w = jnp.where(r == 2 * c, 0.5, 0.0) + jnp.where(jnp.abs(r - 2 * c) == 1, 0.25, 0.0)
    w = jnp.where((c < count) & (r < 2 * count), w, 0.0)
    if wrap is not None:
        w = w + jnp.where((r == wrap) & (c == 0), 0.25, 0.0)
    return w.astype(jnp.bfloat16)


def prolong_matrix(rows, cols, count):
    r, c = iotas((rows, cols))
    w = jnp.where(c == 2 * r, 1.0, 0.0)
    w = w + jnp.where((c == 2 * r + 1) | (c == 2 * r - 1), 0.5, 0.0)
    return jnp.where(r < count, w, 0.0).astype(jnp.bfloat16)


def lane_pad(z):
    return max(z, LANES)


def turn(by):
    return by % LANES if isinstance(by, int) else lax.rem(by, LANES)


def tile_up(h, width):
    return jnp.concatenate([h] * (width // LANES), 1) if width > LANES else h


def buffers(dims):
    f32 = jnp.float32
    out = {}
    rounds = (5, 4, COARSE_SWEEPS - 1)
    for l, (x, y, z) in enumerate(dims):
        zl = lane_pad(z)
        for name in "AB":
            out[f"{name}{l}"] = (x, y, zl)
        if l:
            out[f"G{l}"] = (x, y, zl)
        out[f"yp{l}"] = (2, x, zl)
        out[f"zp{l}"] = (2, y, LANES)
        out[f"hx{l}"] = (rounds[l], 2, y, zl)
        out[f"hy{l}"] = (rounds[l], 2, x, zl)
        out[f"hz{l}"] = (rounds[l], 2, y, LANES)
        for kind in (["r"] if l < 2 else []) + (["p"] if l else []):
            out[f"{kind}x{l}"] = (y, zl)
            out[f"{kind}y{l}"] = (x + 8, zl)
            out[f"{kind}z{l}"] = (y + 8, LANES)
            out[f"{kind}w{l}"] = (y + 8, LANES)
        if l < 2:
            out[f"T{l}"] = (x // 2, y // 2, zl)
            out[f"S{l}"] = (zl // LANES, y, LANES)
            out[f"TH{l}"] = (y // 2, zl)
            out[f"TY{l}"] = (x // 2 + 8, zl)
        out[f"M{l}"] = (y + 8, LANES)
        out[f"N{l}"] = (y, LANES)
    return {k: pltpu.VMEM(v, f32) for k, v in out.items()}


def kernel(dims, counts, names, cells, u_far, f_far, out, *scratch):
    b = dict(zip(names, scratch[:-3]))
    send_sem, recv_sem, load_sem = scratch[-3:]
    u, f = b["u"], b["f"]
    load_u = pltpu.make_async_copy(u_far, u, load_sem.at[0])
    load_f = pltpu.make_async_copy(f_far, f, load_sem.at[1])
    load_u.start()
    load_f.start()
    here = {a: lax.axis_index(a) for a in AXES}
    serial = itertools.count()

    def device(offset):
        return tuple(lax.rem(here[a] + (o % n), n) for a, o, n in zip(AXES, offset, counts))

    def copy(src, dst, offset):
        k = next(serial)
        c = pltpu.make_async_remote_copy(
            src_ref=src,
            dst_ref=dst,
            send_sem=send_sem.at[k],
            recv_sem=recv_sem.at[k],
            device_id=device(offset),
            device_id_type=pl.DeviceIdType.MESH,
        )
        c.start()
        return c

    def wait(copies):
        for c in copies:
            c.wait()

    offsets = []
    for sign in (1, -1):
        for o in itertools.product((0, 1), repeat=3):
            if any(o):
                offsets.append(tuple(sign * v for v in o))
    for a in range(3):
        for j in range(2, counts[a] - 1):
            offsets.append(tuple(j if i == a else 0 for i in range(3)))
    barrier = pltpu.get_barrier_semaphore()
    for o in offsets:
        pl.semaphore_signal(
            barrier, inc=1, device_id=device(o), device_id_type=pl.DeviceIdType.MESH
        )
    pl.semaphore_wait(barrier, len(offsets))

    def exchange(l, r, v):
        x = dims[l][0]
        hx, hy, hz = (b[f"h{a}{l}"] for a in "xyz")
        yp, zp = b[f"yp{l}"], b[f"zp{l}"]

        def early():
            return [
                copy(v.at[x - 1], hx.at[r, 0], (1, 0, 0)),
                copy(v.at[0], hx.at[r, 1], (-1, 0, 0)),
            ]

        def late():
            return [
                copy(yp.at[1], hy.at[r, 0], (0, 1, 0)),
                copy(yp.at[0], hy.at[r, 1], (0, -1, 0)),
                copy(zp.at[1], hz.at[r, 0], (0, 0, 1)),
                copy(zp.at[0], hz.at[r, 1], (0, 0, -1)),
            ]

        return early, late

    def corner_exchange(kind, l, v):
        x, y, _ = dims[l]
        hi = kind == "r"
        s = 1 if hi else -1
        side = 1 if hi else 0
        yp, zp = b[f"yp{l}"].at[side], b[f"zp{l}"].at[side]
        hx, hy, hz, hw = (b[f"{kind}{a}{l}"] for a in "xyzw")
        ye = yp.at[pl.ds(x - 8 if hi else 0, 8)]
        ze = zp.at[pl.ds(y - 8 if hi else 0, 8)]

        def early():
            return [copy(v.at[x - 1 if hi else 0], hx, (s, 0, 0))]

        def late():
            return [
                copy(ze, hw.at[pl.ds(y, 8)], (s, s, s)),
                copy(zp, hw.at[pl.ds(0, y)], (s, 0, s)),
                copy(ze, hz.at[pl.ds(y, 8)], (0, s, s)),
                copy(ye, hy.at[pl.ds(x, 8)], (s, s, 0)),
                copy(yp, hy.at[pl.ds(0, x)], (0, s, 0)),
                copy(zp, hz.at[pl.ds(0, y)], (0, 0, s)),
            ]

        return early, late

    def both(parts):
        return parts[0]() + parts[1]()

    def zero_acc(l):
        z = jnp.zeros((dims[l][1], LANES), jnp.float32)
        return (z, z)

    def pack(l, x, new, acc):
        _, y, z = dims[l]
        yp = b[f"yp{l}"]
        yp[0, pl.ds(x, 1), :] = new[:1]
        yp[1, pl.ds(x, 1), :] = new[y - 1 :]
        lane = lax.broadcasted_iota(jnp.int32, (y, LANES), 1)
        last = (z - 1) % LANES
        low = pltpu.roll(new[:, :LANES], x, 1)
        high = pltpu.roll(new[:, -LANES:], turn(x + (LANES - last)), 1)
        return (jnp.where(lane == x, low, acc[0]), jnp.where(lane == x, high, acc[1]))

    def store_acc(l, acc):
        b[f"zp{l}"][0] = acc[0]
        b[f"zp{l}"][1] = acc[1]

    def planes(l, body, packed=True):
        def step(i, acc):
            new = body(i)
            return pack(l, i, new, acc) if packed else acc

        acc = lax.fori_loop(0, dims[l][0], step, zero_acc(l))
        if packed:
            store_acc(l, acc)

    def sweep(l, r, moving, src, dst, g, onward=None, defect=False, shift=None):
        x, y, z = dims[l]
        zl = lane_pad(z)
        scale = 0.25**l
        hx, hy, hz = (b[f"h{a}{l}"].at[r] for a in "xyz")
        row, lane = iotas((y, zl))
        last = (z - 1) % LANES
        gain = scale if defect else relax_weight / 6.0

        def plane(i, around):
            c = src[i]
            up = jnp.where(row == 0, 0.0, pltpu.roll(c, 1, 0))
            down = jnp.where(row == y - 1, 0.0, pltpu.roll(c, y - 1, 0))
            left = jnp.where(lane == 0, 0.0, pltpu.roll(c, 1, 1))
            right = jnp.where(lane == z - 1, 0.0, pltpu.roll(c, zl - 1, 1))
            beside = around + (up + down) + (left + right)
            if defect:
                new = g[i] - scale * (6.0 * c - beside)
            else:
                new = (1.0 - relax_weight) * c + (relax_weight / 6.0) * beside
                new = new + (relax_weight / (6.0 * scale)) * g[i]
                if shift is not None:
                    new = new - shift
            dst[i] = new

        def inner(i, _):
            plane(i, src[i - 1] + src[i + 1])
            return 0

        plane(0, src[1])
        lax.fori_loop(1, x - 1, inner, 0)
        plane(x - 1, src[x - 2])
        wait(moving)
        row8 = lax.broadcasted_iota(jnp.int32, (8, zl), 0)
        lane1 = lax.broadcasted_iota(jnp.int32, (y, LANES), 1)

        def fix(i, acc, beyond=None):
            new = dst[i]
            if beyond is not None:
                new = new + gain * beyond
            top = new[:8] + jnp.where(row8 == 0, gain * hy[0, pl.ds(i, 1), :], 0.0)
            new = jnp.concatenate([top, new[8:]], 0) if y > 8 else top
            end = new[y - 8 :] + jnp.where(row8 == 7, gain * hy[1, pl.ds(i, 1), :], 0.0)
            new = jnp.concatenate([new[: y - 8], end], 0) if y > 8 else end
            parts = halves(new)
            left = pltpu.roll(hz[0], turn(LANES - i), 1)
            right = pltpu.roll(hz[1], turn(LANES + last - i), 1)
            parts[0] = parts[0] + jnp.where(lane1 == 0, gain * left, 0.0)
            parts[-1] = parts[-1] + jnp.where(lane1 == last, gain * right, 0.0)
            new = jnp.concatenate(parts, 1) if len(parts) > 1 else parts[0]
            dst[i] = new
            return pack(l, i, new, acc) if onward is not None else acc

        acc = fix(0, zero_acc(l), hx[0])
        acc = fix(x - 1, acc, hx[1])
        started = onward[0]() if onward is not None else []
        acc = lax.fori_loop(1, x - 1, fix, acc)
        if onward is not None:
            store_acc(l, acc)
            started = started + onward[1]()
        return started

    def halves(v):
        return [v[:, k : k + LANES] for k in range(0, v.shape[1], LANES)]

    def restrict_y(ref, row_before):
        n = ref.shape[1] // 2
        parts = []
        first = lax.broadcasted_iota(jnp.int32, (n, LANES), 0) == 0
        for t, rim in enumerate(halves(row_before)):
            even = ref[t, pl.ds(0, n, stride=2), :]
            odd = ref[t, pl.ds(1, n, stride=2), :]
            below = jnp.where(first, rim, pltpu.roll(odd, 1, 0))
            parts.append(0.25 * below + 0.5 * even + 0.25 * odd)
        return jnp.concatenate(parts, 1) if len(parts) > 1 else parts[0]

    def restrict_down(l, d, mean):
        x, y, z = dims[l]
        zl = lane_pad(z)
        xc, yc, zc = dims[l + 1]
        zlc = lane_pad(zc)
        hx, hy, hz, hw = (b[f"r{a}{l}"] for a in "xyzw")
        s, t = b[f"S{l}"], b[f"T{l}"]
        m, n = b[f"M{l}"], b[f"N{l}"]
        lane = lax.broadcasted_iota(jnp.int32, (y + 8, LANES), 1)
        moved = pltpu.roll(hw[...], LANES - x, 1)
        rim = jnp.where(lane == LANES - 1, moved, hz[...])
        m[...] = dot_exact(rim, restrict_matrix(LANES, LANES, xc, LANES - 1))
        n[...] = m[pl.ds(0, y), :]
        even = n[pl.ds(0, yc, stride=2), :]
        odd = n[pl.ds(1, yc, stride=2), :]
        first = lax.broadcasted_iota(jnp.int32, (yc, LANES), 0) == 0
        below = jnp.where(first, m[pl.ds(y + 7, 1), :], pltpu.roll(odd, 1, 0))
        n[pl.ds(0, yc), :] = 0.25 * (0.25 * below + 0.5 * even + 0.25 * odd)

        def plane(i, before, before_row):
            dx = 0.25 * before + 0.5 * d[2 * i] + 0.25 * d[2 * i + 1]
            for k, part in enumerate(halves(dx)):
                s[k] = part
            rows = 0.25 * before_row + 0.5 * hy[pl.ds(2 * i, 1), :]
            rows = rows + 0.25 * hy[pl.ds(2 * i + 1, 1), :]
            t[i] = restrict_y(s, rows)

        def inner(i, _):
            plane(i, d[2 * i - 1], hy[pl.ds(2 * i - 1, 1), :])
            return 0

        plane(0, hx[...], hy[pl.ds(x + 7, 1), :])
        lax.fori_loop(1, xc, inner, 0)
        g, v = b[f"G{l + 1}"], b[f"A{l + 1}"]
        w = restrict_matrix(zl, zlc, zc)
        chunk = 8

        def multiply(k, _):
            rows = t[pl.ds(k * chunk, chunk)].reshape(chunk * yc, zl)
            g[pl.ds(k * chunk, chunk)] = dot_exact(rows, w).reshape(chunk, yc, zlc)
            return 0

        lax.fori_loop(0, xc // chunk, multiply, 0)
        lane_c = lax.broadcasted_iota(jnp.int32, (yc, zlc), 1)

        def finish(i):
            col = pltpu.roll(n[pl.ds(0, yc), :], turn(LANES - i), 1)
            new = g[i] + jnp.where(lane_c == 0, tile_up(col, zlc), 0.0)
            if mean is not None:
                new = new - mean
            g[i] = new
            new = (relax_weight / (6.0 * 0.25 ** (l + 1))) * new
            v[i] = new
            return new

        planes(l + 1, finish)

    def prolong_up(l, c, v, work, shift):
        x, y, z = dims[l]
        zl = lane_pad(z)
        xc, yc, zc = dims[l + 1]
        zlc = lane_pad(zc)
        hx, hy, hz, hw = (b[f"p{a}{l + 1}"] for a in "xyzw")
        s, t, th, ty = b[f"S{l}"], b[f"T{l}"], b[f"TH{l}"], b[f"TY{l}"]
        m = b[f"M{l + 1}"]
        lane = lax.broadcasted_iota(jnp.int32, (yc + 8, LANES), 1)
        m[...] = 0.5 * jnp.where(lane == xc, pltpu.roll(hw[...], xc, 1), hz[...])
        w = prolong_matrix(zlc, zl, zc)
        chunk = 8

        def multiply(k, _):
            rows = c[pl.ds(k * chunk, chunk)].reshape(chunk * yc, zlc)
            t[pl.ds(k * chunk, chunk)] = dot_exact(rows, w).reshape(chunk, yc, zl)
            return 0

        lax.fori_loop(0, xc // chunk, multiply, 0)
        th[...] = dot_exact(hx[...], w)
        ty[...] = dot_exact(hy[...], w)
        at_end = lane == LANES - 1
        final = lax.broadcasted_iota(jnp.int32, (yc, LANES), 0) == yc - 1

        def plane(i, values):
            add = pltpu.roll(m[...], turn(2 * LANES - 1 - i), 1)
            add = jnp.where(at_end, add, 0.0)
            rim = ty[pl.ds(i, 1), :]
            rims, parts = halves(rim), halves(values)
            parts[-1] = parts[-1] + add[:yc]
            rims[-1] = rims[-1] + add[yc : yc + 1]
            for k, (part, edge) in enumerate(zip(parts, rims)):
                above = jnp.where(final, edge, pltpu.roll(part, yc - 1, 0))
                s[k, pl.ds(0, yc, stride=2), :] = part
                s[k, pl.ds(1, yc, stride=2), :] = 0.5 * (part + above)
            full = [s[k] for k in range(len(parts))]
            work[i] = jnp.concatenate(full, 1) if len(full) > 1 else full[0]

        def spread(i, _):
            plane(i, t[i])
            return 0

        lax.fori_loop(0, xc, spread, 0)
        plane(xc, th[...])

        def add(i, acc):
            low, high = work[i], work[i + 1]
            if shift is not None:
                low, high = low - shift, high - shift
            even = v[2 * i] + low
            odd = v[2 * i + 1] + 0.5 * (low + high)
            v[2 * i] = even
            v[2 * i + 1] = odd
            return pack(l, 2 * i + 1, odd, pack(l, 2 * i, even, acc))

        store_acc(l, lax.fori_loop(0, xc, add, zero_acc(l)))

    st, sg = b["stats"], [b[f"sums{a}"] for a in range(3)]

    def spread_sums(a):
        return [
            copy(st.at[a], sg[a].at[j], tuple(j if i == a else 0 for i in range(3)))
            for j in range(1, counts[a])
        ]

    def gather_sums(a, copies):
        wait(copies)
        total = st[a]
        for j in range(1, counts[a]):
            total = total + sg[a][j]
        if a < 2:
            st[a + 1] = total
        return total

    x0, y0, z0 = dims[0]

    def folded(v):
        return jnp.sum(v.reshape(y0 // 8, 8, z0), 0)

    def first(i, carry):
        total, acc = carry
        v = u[i]
        return total + folded(v), pack(0, i, v, acc)

    none = jnp.zeros((8, z0), jnp.float32)
    load_u.wait()
    total_u, acc = lax.fori_loop(0, x0, first, (none, zero_acc(0)))
    store_acc(0, acc)
    moving = both(exchange(0, 0, u))
    load_f.wait()
    total_f = lax.fori_loop(0, x0, lambda i, t: t + folded(f[i]), none)
    st[0, 0] = total_u
    st[0, 1] = total_f
    sums = spread_sums(0)
    a0, b0, a1, b1 = b["A0"], b["B0"], b["A1"], b["B1"]
    a2, b2 = b["A2"], b["B2"]
    g1, g2 = b["G1"], b["G2"]
    moving = sweep(0, 0, moving, u, a0, f, exchange(0, 1, a0))
    gather_sums(0, sums)
    sums = spread_sums(1)
    moving = sweep(0, 1, moving, a0, b0, f, exchange(0, 2, b0))
    gather_sums(1, sums)
    sums = spread_sums(2)
    moving = sweep(0, 2, moving, b0, a0, f, corner_exchange("r", 0, a0), defect=True)
    total = gather_sums(2, sums)
    mean_u = jnp.sum(total[0]) * (1.0 / cells)
    mean_f = jnp.sum(total[1]) * (1.0 / cells)
    gain = relax_weight / 6.0
    wait(moving)
    restrict_down(0, a0, mean_f)

    moving = both(exchange(1, 0, a1))
    moving = sweep(1, 0, moving, a1, b1, g1, exchange(1, 1, b1))
    moving = sweep(1, 1, moving, b1, a1, g1, corner_exchange("r", 1, a1), defect=True)
    wait(moving)
    restrict_down(1, a1, None)

    v, w = a2, b2
    moving = both(exchange(2, 0, v))
    for k in range(COARSE_SWEEPS - 1):
        final = k == COARSE_SWEEPS - 2
        onward = corner_exchange("p", 2, w) if final else exchange(2, k + 1, w)
        moving = sweep(2, k, moving, v, w, g2, onward)
        v, w = w, v
    wait(moving)
    prolong_up(1, v, b1, a1, None)
    moving = both(exchange(1, 2, b1))
    moving = sweep(1, 2, moving, b1, a1, g1, exchange(1, 3, a1))
    moving = sweep(1, 3, moving, a1, b1, g1, corner_exchange("p", 1, b1))
    wait(moving)
    prolong_up(0, b1, b0, a0, mean_u + 2.0 * gain * mean_f)
    moving = both(exchange(0, 3, b0))
    moving = sweep(0, 3, moving, b0, a0, f, exchange(0, 4, a0), shift=gain * mean_f)
    sweep(0, 4, moving, a0, out, f, shift=gain * mean_f)


def solution(mesh):
    counts = tuple(mesh.shape[a] for a in AXES)

    def shards(right_side, initial_guess):
        shape = right_side.shape
        dims = tuple(tuple(n >> l for n in shape) for l in range(3))
        cells = float(right_side.size)
        for n in counts:
            cells *= n
        bufs = buffers(dims)
        bufs["u"] = pltpu.VMEM(shape, jnp.float32)
        bufs["f"] = pltpu.VMEM(shape, jnp.float32)
        bufs["stats"] = pltpu.VMEM((3, 2, 8, shape[2]), jnp.float32)
        for a in range(3):
            bufs[f"sums{a}"] = pltpu.VMEM((counts[a], 2, 8, shape[2]), jnp.float32)
        messages = 6 * (9 + COARSE_SWEEPS - 1) + 7 * 4 + sum(counts) - 3
        vmem = pl.BlockSpec(memory_space=pltpu.VMEM)
        return pl.pallas_call(
            functools.partial(kernel, dims, counts, tuple(bufs), cells),
            out_shape=jax.ShapeDtypeStruct(shape, jnp.float32),
            in_specs=[pl.BlockSpec(memory_space=pl.ANY)] * 2,
            out_specs=vmem,
            scratch_shapes=list(bufs.values())
            + [pltpu.SemaphoreType.DMA((n,)) for n in (messages, messages, 2)],
            compiler_params=pltpu.CompilerParams(
                collective_id=0, has_side_effects=True, vmem_limit_bytes=48 * 1024 * 1024
            ),
        )(initial_guess, right_side)

    placed = (P(*AXES), P(*AXES))
    return jax.shard_map(
        shards, mesh=mesh, in_specs=placed, out_specs=P(*AXES), check_vma=False
    )
```

profile of v0, /device:TPU:0, one launch (start us, length us, event | category | flops | bytes accessed | tf_op | source)
XLA Modules:
  0.0 195.4 jit_solution(15568199373817410917)
XLA Ops:
  0.0 193.4 %shard_map.28 = f32[64,64,256]{2,1,0:T(8,128)S(1)} custom-call(f32[64,64,256]{2,1,0:T(8,128)} %u_far.1, f32[64,64,256]{2,1,0:T(8,128)} %f_far.1), custom_call_target="tpu_custom_call" | custom-call | tf_op jit(solution)/shard_map/pallas_call | solution.py:500
  193.4 2.0 %copy.4 = f32[64,64,256]{2,1,0:T(8,128)} copy(f32[64,64,256]{2,1,0:T(8,128)S(1)} %shard_map.28) | data formatting | bytes 8388608
where the time goes:
time: 196 us; the launch traced here: 195 us
  Pallas kernels  193 us (98%)
  local copies, waits for them, and re-layouts  2.02 us (1%)
    pallas_call x1, Pallas kernels, shards(): pl.pallas_call(functools.partial(kernel, dims, counts, tuple(bufs), cells...  193 us

commit v1 on v0

v1 whole, which is shorter than its diff:
```python
import functools
import itertools

import jax
import jax.numpy as jnp
from jax import lax
from jax.experimental import pallas as pl
from jax.experimental.pallas import tpu as pltpu
from jax.sharding import PartitionSpec as P

COARSE_SWEEPS = 6
LANES = 128
AXES = ("gx", "gy", "gz")
relax_weight = 0.8
W = relax_weight / 6.0

HALO1 = (3, 4)
HALO2 = (COARSE_SWEEPS, COARSE_SWEEPS + 1)


def dot_exact(a, w):
    hi = a.astype(jnp.bfloat16)
    rest = a - hi.astype(jnp.float32)
    mid = rest.astype(jnp.bfloat16)
    low = (rest - mid.astype(jnp.float32)).astype(jnp.bfloat16)
    dot = functools.partial(jnp.dot, preferred_element_type=jnp.float32)
    return dot(hi, w) + (dot(mid, w) + dot(low, w))


def iotas(shape):
    return (
        lax.broadcasted_iota(jnp.int32, shape, 0),
        lax.broadcasted_iota(jnp.int32, shape, 1),
    )


def restrict_matrix(rows, cols, count, wrap=None, step=1):
    r, c = iotas((rows, cols))
    d = jnp.abs(r - 2 * step * c)
    w = jnp.where(d == 0, 0.5, 0.0) + jnp.where(d == step, 0.25, 0.0)
    w = jnp.where((c < count) & (r < 2 * step * count), w, 0.0)
    if wrap is not None:
        w = w + jnp.where((r == wrap) & (c == 0), 0.25, 0.0)
    return w.astype(jnp.bfloat16)


def prolong_matrix(rows, cols, fine, wrapped):
    r, c = iotas((rows, cols))
    if wrapped:
        r = jnp.where(r < 3 * rows // 4, r, r - rows)
        c = jnp.where(c < 3 * cols // 4, c, c - cols)
    d = jnp.abs(c - 2 * r)
    w = jnp.where(d == 0, 1.0, 0.0) + jnp.where(d == 1, 0.5, 0.0)
    return w.astype(jnp.bfloat16)


def turn(by):
    return by % LANES if isinstance(by, int) else lax.rem(by, LANES)


def extended(dims):
    (x1, y1, _), (x2, y2, _) = dims[1], dims[2]
    up = lambda n: -(-n // 8) * 8
    return (
        None,
        (x1 + sum(HALO1), up(y1 + sum(HALO1)), 2),
        (x2 + sum(HALO2), up(y2 + sum(HALO2)), 1),
    )


def buffers(dims, counts):
    (x, y, z), (x1, y1, _), (x2, y2, _) = dims
    ext = extended(dims)
    out = {}
    out["u"] = (x, y, z)
    out["f"] = (x, y, z)
    out["A0"] = (x + 1, y + 8, z)
    out["B0"] = (x, y, z)
    out["yp"] = (2, 2, x, z)
    out["zp"] = (2, y, LANES)
    out["zh"] = (y, LANES)
    out["hx"] = (5, 2, y, z)
    out["hy"] = (5, 2, x, z)
    out["hz"] = (5, 2, y, LANES)
    out["rz"] = (y + 8, LANES)
    out["rw"] = (y + 8, LANES)
    out["m"] = (y + 8, LANES)
    out["n"] = (y // 2, LANES)
    out["S"] = (4, z // LANES, y + 8, LANES)
    out["T0"] = (x1, y1, z)
    out["T1"] = (x2, y2, ext[1][2] * LANES)
    for l, n in ((1, (x1, y1)), (2, (x2, y2))):
        ex, ey, tiles = ext[l]
        for name in "GAB":
            out[f"{name}{l}"] = (ex, ey, tiles * LANES)
        out[f"zp{l}"] = (2, n[1], LANES)
        out[f"hz{l}"] = (2, 4, ey, LANES)
    out["Q1"] = (ext[2][0], ext[2][1], 2 * LANES)
    out["V1"] = (ext[2][0], 2, 2 * ext[2][1], LANES)
    out["Q0"] = (x1 + 1, ext[1][1], z)
    out["V0"] = (x1 + 1, z // LANES, y, LANES)
    out["stats"] = (3, 2, 8, LANES)
    for a in range(3):
        out[f"sums{a}"] = (counts[a], 2, 8, LANES)
    return {k: pltpu.VMEM(v, jnp.float32) for k, v in out.items()}


def kernel(dims, counts, names, cells, u_far, f_far, out, *scratch):
    b = dict(zip(names, scratch[:-3]))
    send_sem, recv_sem, load_sem = scratch[-3:]
    u, f, a0, b0 = b["u"], b["f"], b["A0"], b["B0"]
    load_u = pltpu.make_async_copy(u_far, u, load_sem.at[0])
    load_f = pltpu.make_async_copy(f_far, f, load_sem.at[1])
    load_u.start()
    load_f.start()
    here = {a: lax.axis_index(a) for a in AXES}
    serial = itertools.count()
    ext = extended(dims)
    x0, y0, z0 = dims[0]
    x1, y1, z1 = dims[1]
    x2, y2, z2 = dims[2]
    nb0, nt0 = y0 // 8, z0 // LANES
    assert 2 * x0 == LANES and z1 == LANES and 2 * z2 == LANES
    assert nt0 == 2 and y2 % 8 == 0

    def device(offset):
        return tuple(lax.rem(here[a] + (o % n), n) for a, o, n in zip(AXES, offset, counts))

    def copy(src, dst, offset):
        k = next(serial)
        c = pltpu.make_async_remote_copy(
            src_ref=src,
            dst_ref=dst,
            send_sem=send_sem.at[k],
            recv_sem=recv_sem.at[k],
            device_id=device(offset),
            device_id_type=pl.DeviceIdType.MESH,
        )
        c.start()
        return c

    def wait(copies):
        with jax.named_scope("wait"):
            for c in copies:
                c.wait()

    around = [o for o in itertools.product((-1, 0, 1), repeat=3) if any(o)]
    offsets = list(around)
    for a in range(3):
        for j in range(2, counts[a] - 1):
            offsets.append(tuple(j if i == a else 0 for i in range(3)))
    barrier = pltpu.get_barrier_semaphore()
    for o in offsets:
        pl.semaphore_signal(
            barrier, inc=1, device_id=device(o), device_id_type=pl.DeviceIdType.MESH
        )

    row8 = lax.broadcasted_iota(jnp.int32, (8, LANES), 0)
    lane8 = lax.broadcasted_iota(jnp.int32, (8, LANES), 1)
    zero8 = jnp.zeros((8, LANES), jnp.float32)

    def tile(k, t):
        return pl.ds(8 * k, 8), pl.ds(LANES * t, LANES)

    def at(i, k, t):
        return (i,) + tile(k, t)

    def groups(lo, hi, size, body):
        steps = (hi - lo) // size

        def step(p, _):
            body(lo + size * p, size)
            return 0

        if steps > 1:
            lax.fori_loop(0, steps, step, 0)
        elif steps:
            body(lo, size)
        if (hi - lo) % size:
            body(lo + size * steps, (hi - lo) % size)

    def stencil(mode, l, src, g, i, near, nb, nt, wrap, shift=None):
        scale = 0.25**l
        c = [[src[at(i, k, t)] for t in range(nt)] for k in range(nb)]
        up = [[pltpu.roll(v, 1, 0) for v in p] for p in c]
        down = [[pltpu.roll(v, 7, 0) for v in p] for p in c]
        new = []
        for k in range(nb):
            left = [pltpu.roll(v, 1, 1) for v in c[k]]
            right = [pltpu.roll(v, LANES - 1, 1) for v in c[k]]
            line = []
            for t in range(nt):
                v = c[k][t]
                above = up[k - 1][t] if k or wrap else 0.0
                below = down[(k + 1) % nb][t] if k < nb - 1 or wrap else 0.0
                s = jnp.where(row8 == 0, above, up[k][t])
                s = s + jnp.where(row8 == 7, below, down[k][t])
                if wrap and nt == 1:
                    s = s + left[t] + right[t]
                else:
                    before = left[t - 1] if t or wrap else 0.0
                    after = right[(t + 1) % nt] if t < nt - 1 or wrap else 0.0
                    s = s + jnp.where(lane8 == 0, before, left[t])
                    s = s + jnp.where(lane8 == LANES - 1, after, right[t])
                for j in near:
                    s = s + src[at(j, k, t)]
                if mode == "first":
                    z = W / scale
                    value = (W * z) * s + (W * (1.5 * z + 1.0 / scale)) * v
                elif mode == "defect":
                    value = s - 6.0 * v
                    value = g[at(i, k, t)] + (value if l == 0 else scale * value)
                else:
                    gv = g[at(i, k, t)]
                    value = s + 1.5 * v
                    value = value + (gv if l == 0 else (1.0 / scale) * gv)
                    value = W * value
                    if shift is not None:
                        value = value - shift
                line.append(value)
            new.append(line)
        return new

    def put(dst, i, new):
        for k, line in enumerate(new):
            for t, value in enumerate(line):
                dst[at(i, k, t)] = value

    zh = b["zh"]
    last = LANES - 1

    def pack_z(zp, i, ref, blocks=range(nb0)):
        moved = []
        for k in blocks:
            both = jnp.where(lane8 == last, ref[at(i, k, nt0 - 1)], ref[at(i, k, 0)])
            moved.append(pltpu.roll(both, turn(2 * i + 1), 1))
        mask = (lane8 == 2 * i) | (lane8 == 2 * i + 1)
        for k, v in zip(blocks, moved):
            pltpu.store(zp.at[pl.ds(8 * k, 8), :], v, mask=mask)

    def pack_rows(yp, i, new):
        for side, (k, r) in enumerate(((0, 0), (nb0 - 1, 7))):
            yp[side, pl.ds(i, 1), :] = jnp.concatenate([v[r : r + 1] for v in new[k]], 1)

    def exchange(r, src, yl, yh):
        hx, hy, hz = b["hx"].at[r], b["hy"].at[r], b["hz"].at[r]
        zp = b["zp"].at[r % 2]
        rows = pl.ds(0, y0)

        def send_x(ref=None):
            ref = src if ref is None else ref
            return [
                copy(ref.at[x0 - 1, rows], hx.at[0], (1, 0, 0)),
                copy(ref.at[0, rows], hx.at[1], (-1, 0, 0)),
            ]

        def send_y():
            return [
                copy(yh, hy.at[0], (0, 1, 0)),
                copy(yl, hy.at[1], (0, -1, 0)),
            ]

        def send_z():
            return [
                copy(zp, hz.at[0], (0, 0, 1)),
                copy(zp, hz.at[1], (0, 0, -1)),
            ]

        return send_x, send_y, send_z

    def defect_exchange(r, d):
        rz, rw = b["rz"], b["rw"]
        yp, zp = b["yp"].at[r % 2], b["zp"].at[r % 2]

        def send_x():
            return [copy(d.at[x0 - 1, pl.ds(0, y0)], d.at[x0, pl.ds(0, y0)], (1, 0, 0))]

        def send_y():
            return [
                copy(yp.at[1, x0 - 1], d.at[x0, y0 + 7], (1, 1, 0)),
                copy(yp.at[1], d.at[pl.ds(0, x0), y0 + 7], (0, 1, 0)),
            ]

        def send_z():
            end, all_rows = zp.at[pl.ds(y0 - 1, 1)], pl.ds(8, y0)
            return [
                copy(end, rw.at[pl.ds(7, 1)], (1, 1, 1)),
                copy(zp, rw.at[all_rows], (1, 0, 1)),
                copy(end, rz.at[pl.ds(7, 1)], (0, 1, 1)),
                copy(zp, rz.at[all_rows], (0, 0, 1)),
            ]

        return send_x, send_y, send_z

    def sweep(r, moving, src, dst, onward=None, mode="relax", shift=None):
        hx, hy, hz = b["hx"].at[r], b["hy"].at[r], b["hz"].at[r]
        yp, zp = b["yp"].at[(r + 1) % 2], b["zp"].at[(r + 1) % 2]
        gain = 1.0 if mode == "defect" else W
        packed = onward is not None

        def plane(i, near):
            new = stencil(mode, 0, src, f, i, near, nb0, nt0, False, shift)
            put(dst, i, new)
            if packed:
                pack_rows(yp, i, new)

        def pair(p, _):
            i = 1 + 2 * p
            plane(i, (i - 1, i + 1))
            plane(i + 1, (i, i + 2))
            if packed:
                pack_z(zp, i - 2, dst)
                pack_z(zp, i - 1, dst)
            return 0

        with jax.named_scope("inner"):
            plane(0, (1,))
            plane(x0 - 1, (x0 - 2,))
            plane(1, (0, 2))
            plane(2, (1, 3))
            lax.fori_loop(1, (x0 - 2) // 2, pair, 0)
            if packed:
                pack_z(zp, x0 - 3, dst)
                pack_z(zp, x0 - 2, dst)
        wait(moving)
        odd = lane8 % 2 == 1
        for k in range(nb0):
            rows = pl.ds(8 * k, 8)
            before = pltpu.roll(hz[0, rows, :], 1, 1)
            after = pltpu.roll(hz[1, rows, :], LANES - 1, 1)
            zh[rows, :] = gain * jnp.where(odd, before, after)

        def fix(i, size, beyond=None):
            done = []
            for p in range(i, i + size) if isinstance(i, int) else [i + q for q in range(size)]:
                edges = [gain * hy[s, pl.ds(p, 1), :] for s in range(2)]
                for k in range(nb0):
                    halo = pltpu.roll(zh[pl.ds(8 * k, 8), :], turn(2 * LANES - 2 * p - 1), 1)
                    inside = 0 < k < nb0 - 1 and beyond is None
                    for t in (0, nt0 - 1) if inside else range(nt0):
                        v = dst[at(p, k, t)]
                        if beyond is not None:
                            v = v + gain * beyond[tile(k, t)]
                        for s, kk, rr in ((0, 0, 0), (1, nb0 - 1, 7)):
                            if k == kk:
                                edge = edges[s][:, LANES * t : LANES * t + LANES]
                                v = v + jnp.where(row8 == rr, edge, 0.0)
                        if t == 0:
                            v = v + jnp.where(lane8 == 0, halo, 0.0)
                        if t == nt0 - 1:
                            v = v + jnp.where(lane8 == last, halo, 0.0)
                        done.append((at(p, k, t), v))
            for where, v in done:
                dst[where] = v

        with jax.named_scope("ends"):
            fix(0, 1, hx.at[0])
            fix(x0 - 1, 1, hx.at[1])
        if not packed:
            with jax.named_scope("fix"):
                groups(1, x0 - 1, 4, fix)
            return []
        started = onward[0]()
        with jax.named_scope("yface"):
            for side, r0 in ((0, 0), (1, y0 - 1)):
                line = jnp.broadcast_to(zh[pl.ds(r0, 1), :], (8, LANES))
                for j in range(x0 // 8):
                    slot = 2 * (8 * j + row8)
                    low = jnp.sum(jnp.where(lane8 == slot + 1, line, 0.0), 1, keepdims=True)
                    high = jnp.sum(jnp.where(lane8 == slot, line, 0.0), 1, keepdims=True)
                    for t in range(nt0):
                        rows = (side,) + tile(j, t)
                        v = yp[rows] + gain * hy[rows]
                        if t == 0:
                            v = v + jnp.where(lane8 == 0, low, 0.0)
                        if t == nt0 - 1:
                            v = v + jnp.where(lane8 == last, high, 0.0)
                        yp[rows] = v
                for i in (0, x0 - 1):
                    yp[side, pl.ds(i, 1), :] = dst[i, pl.ds(r0, 1), :]
        started = started + onward[1]()
        with jax.named_scope("zface"):
            for k in range(nb0):
                v = zp[pl.ds(8 * k, 8), :] + zh[pl.ds(8 * k, 8), :]
                for side, kk, rr in ((0, 0, 0), (1, nb0 - 1, 7)):
                    if k == kk:
                        total = zero8
                        for j in range(x0 // 8):
                            slot = 2 * (8 * j + row8)
                            low = hy[(side,) + tile(j, 0)][:, :1]
                            high = hy[(side,) + tile(j, nt0 - 1)][:, last:]
                            total = total + jnp.where(lane8 == slot + 1, low, 0.0)
                            total = total + jnp.where(lane8 == slot, high, 0.0)
                        total = gain * jnp.sum(total, 0, keepdims=True)
                        v = v + jnp.where(row8 == rr, total, 0.0)
                zp[pl.ds(8 * k, 8), :] = v
            pack_z(zp, 0, dst)
            pack_z(zp, x0 - 1, dst)
        started = started + onward[2]()
        with jax.named_scope("fix"):
            groups(1, x0 - 1, 4, fix)
        return started

    def restrict_xy(d, before, j, u_slot, nb, top, nt, dst):
        s = b["S"].at[u_slot]
        low = 2 * j - 1 if before is None else before
        for t in range(nt):
            for q, k in enumerate((top,) + tuple(range(nb))):
                v = 0.25 * (d[at(low, k, t)] + d[at(2 * j + 1, k, t)])
                s[t, pl.ds(8 * q, 8), :] = v + 0.5 * d[at(2 * j, k, t)]
        n = nb * 4
        for t in range(nt):
            v = 0.25 * (s[t, pl.ds(7, n, stride=2), :] + s[t, pl.ds(9, n, stride=2), :])
            dst[j, :, pl.ds(LANES * t, LANES)] = v + 0.5 * s[t, pl.ds(8, n, stride=2), :]

    def restrict_planes(d, before, nb, top, nt, dst, count):
        restrict_xy(d, before, 0, 0, nb, top, nt, dst)
        for j in range(1, 4):
            restrict_xy(d, None, j, j, nb, top, nt, dst)

        def some(p, _):
            for q in range(4):
                restrict_xy(d, None, 4 * p + q, q, nb, top, nt, dst)
            return 0

        lax.fori_loop(1, count // 4, some, 0)

    def multiply(src, dst, w, first, count, chunk, rows, cols):
        zs = src.shape[2]

        def step(k, _):
            i = first + k * chunk if not isinstance(k, int) else first
            v = src[pl.ds(i, chunk), pl.ds(0, rows), :].reshape(chunk * rows, zs)
            v = dot_exact(v, w).reshape(chunk, rows, cols)
            dst[pl.ds(i, chunk), pl.ds(0, rows), pl.ds(0, cols)] = v
            return 0

        if count == chunk:
            step(0, 0)
        else:
            lax.fori_loop(0, count // chunk, step, 0)

    def region(o, n, size, depth):
        lo, hi = depth
        if o == 1:
            return pl.ds(n - lo, lo), pl.ds(size - lo, lo)
        if o == -1:
            return pl.ds(0, hi), pl.ds(n, hi)
        return pl.ds(0, n), pl.ds(0, n)

    def halo_send(l, depth, beside):
        g, zpl, hzl = b[f"G{l}"], b[f"zp{l}"], b[f"hz{l}"]
        nx, ny, _ = dims[l]
        ex, ey, _ = ext[l]
        started = []
        lanes = pl.ds(0, LANES)
        for o in sorted(around, key=lambda v: -sum(map(abs, v))):
            if (o[2] != 0) == beside:
                continue
            sx, dx = region(o[0], nx, ex, depth)
            sy, dy = region(o[1], ny, ey, depth)
            if beside:
                started.append(copy(g.at[sx, sy, lanes], g.at[dx, dy, lanes], o))
            else:
                side = 0 if o[2] == 1 else 1
                half = {0: (0, 2), 1: (1, 1), -1: (0, 1)}[o[0]]
                slot = {0: 0, 1: 2, -1: 3}[o[0]]
                source = zpl.at[pl.ds(*half), sy]
                started.append(copy(source, hzl.at[side, pl.ds(slot, half[1]), dy], o))
        return started

    def halo_pack(l, depth):
        g, zpl = b[f"G{l}"], b[f"zp{l}"]
        nx, ny, nz = dims[l]
        lo, hi = depth
        width, per = lo + hi, nx // 2
        for half in range(2):
            total = [zero8] * (ny // 8)
            for p in range(per):
                first = width * p
                mask = (lane8 >= first) & (lane8 < first + width)
                for k in range(ny // 8):
                    v = g[at(half * per + p, k, 0)]
                    if nz < LANES:
                        v = jnp.where(lane8 < LANES - nz, v, pltpu.roll(v, LANES - nz, 1))
                    v = pltpu.roll(v, first + lo, 1)
                    total[k] = jnp.where(mask, v, total[k])
            for k in range(ny // 8):
                zpl[half, pl.ds(8 * k, 8), :] = total[k]

    def halo_unpack(l, depth):
        g, hzl = b[f"G{l}"], b[f"hz{l}"]
        nx, ny, nz = dims[l]
        ex, ey, tiles = ext[l]
        lo, hi = depth
        width, per = lo + hi, nx // 2
        left = lane8 < lo
        for p in range(1, per):
            left = left | ((lane8 >= width * p) & (lane8 < width * p + lo))
        for slot in range(4):
            for k in range(ey // 8):
                rows = pl.ds(8 * k, 8)
                hzl[0, slot, rows, :] = jnp.where(left, hzl[0, slot, rows, :], hzl[1, slot, rows, :])
        for e in range(ex):
            if e < nx:
                slot, p = e // per, e % per
            elif e < nx + hi:
                slot, p = 3, e - nx
            else:
                slot, p = 2, (nx - ex + e) % per
            back = LANES - (width * p + lo)
            for k in range(ey // 8):
                v = hzl[0, slot, pl.ds(8 * k, 8), :]
                moved = pltpu.roll(v, back % LANES, 1)
                if nz < LANES:
                    high = pltpu.roll(v, (back + nz) % LANES, 1)
                    moved = jnp.where(lane8 < (nz + LANES) // 2, high, moved)
                    g[at(e, k, 0)] = jnp.where(lane8 < nz, g[at(e, k, 0)], moved)
                else:
                    g[at(e, k, tiles - 1)] = moved

    def ext_sweep(mode, l, src, dst, size):
        ex, ey, nt = ext[l]
        nb = ey // 8
        g = b[f"G{l}"]

        def some(i, count):
            for q in range(count):
                p = i + q
                near = ((p - 1) % ex, (p + 1) % ex) if isinstance(p, int) else (p - 1, p + 1)
                put(dst, p, stencil(mode, l, src, g, p, near, nb, nt, True))

        some(0, 1)
        groups(1, ex - 1, size, some)
        some(ex - 1, 1)

    def spread_rows(q, v, j, k, kn, t, slot_k):
        c, n = q[at(j, k, t)], q[at(j, kn, t)]
        below = jnp.where(row8 == 7, pltpu.roll(n, 7, 0), pltpu.roll(c, 7, 0))
        v[j, t, pl.ds(16 * slot_k, 8, stride=2), :] = c
        v[j, t, pl.ds(16 * slot_k + 1, 8, stride=2), :] = 0.5 * (c + below)

    st, sg = b["stats"], [b[f"sums{a}"] for a in range(3)]

    def spread_sums(a):
        return [
            copy(st.at[a], sg[a].at[j], tuple(j if i == a else 0 for i in range(3)))
            for j in range(1, counts[a])
        ]

    def gather_sums(a, copies):
        wait(copies)
        total = st[a]
        for j in range(1, counts[a]):
            total = total + sg[a][j]
        if a < 2:
            st[a + 1] = total
        return total

    def fold(ref):
        def step(p, totals):
            totals = list(totals)
            for q in range(2):
                for k in range(nb0):
                    for t in range(nt0):
                        totals[(2 * k + t) % 4] += ref[at(2 * p + q, k, t)]
            return tuple(totals)

        t = lax.fori_loop(0, x0 // 2, step, (zero8,) * 4)
        return (t[0] + t[1]) + (t[2] + t[3])

    a1, b1, g1 = b["A1"], b["B1"], b["G1"]
    a2, b2, g2 = b["A2"], b["B2"], b["G2"]

    with jax.named_scope("clear"):
        for ref in (g1, g2):
            shape = ref.shape

            def clear(i, _, ref=ref, shape=shape):
                for k in range(shape[1] // 8):
                    for t in range(shape[2] // LANES):
                        ref[at(i, k, t)] = zero8
                return 0

            lax.fori_loop(0, shape[0], clear, 0)
        for l in (1, 2):
            hzl = b[f"hz{l}"]
            for side in range(2):
                for slot in range(4):
                    for k in range(ext[l][1] // 8):
                        hzl[side, slot, pl.ds(8 * k, 8), :] = zero8
    with jax.named_scope("barrier"):
        pl.semaphore_wait(barrier, len(offsets))
    with jax.named_scope("loadu"):
        load_u.wait()
    send_x, send_y, send_z = exchange(0, u, u.at[:, 0, :], u.at[:, y0 - 1, :])
    moving = send_x() + send_y()
    with jax.named_scope("packu"):

        def pack_some(i, count):
            for q in range(count):
                pack_z(b["zp"].at[0], i + q, u)

        groups(0, x0, 8, pack_some)
    moving = moving + send_z()
    with jax.named_scope("sums"):
        st[0, 0] = fold(u)
        load_f.wait()
        st[0, 1] = fold(f)
    sums = spread_sums(0)
    rows = [(b["yp"].at[r % 2, 0], b["yp"].at[r % 2, 1]) for r in range(5)]
    moving = sweep(0, moving, u, a0, exchange(1, a0, *rows[1]))
    gather_sums(0, sums)
    sums = spread_sums(1)
    moving = sweep(1, moving, a0, b0, exchange(2, b0, *rows[2]))
    gather_sums(1, sums)
    sums = spread_sums(2)
    moving = sweep(2, moving, b0, a0, defect_exchange(3, a0), mode="defect")
    total = gather_sums(2, sums)
    mean_u = jnp.sum(total[0]) * (1.0 / cells)
    mean_f = jnp.sum(total[1]) * (1.0 / cells)
    wait(moving)

    with jax.named_scope("restrict0"):
        lane = lax.broadcasted_iota(jnp.int32, (y0 + 8, LANES), 1)
        moved = pltpu.roll(b["rw"][...], 1, 1)
        rim = jnp.where(lane == last, moved, b["rz"][...])
        b["m"][...] = dot_exact(rim, restrict_matrix(LANES, LANES, x1, last, 2))
        m = b["m"]
        v = 0.25 * (m[pl.ds(7, y1, stride=2), :] + m[pl.ds(9, y1, stride=2), :])
        b["n"][...] = 0.25 * (v + 0.5 * m[pl.ds(8, y1, stride=2), :])
        restrict_planes(a0, x0, nb0, nb0, nt0, b["T0"], x1)
        w = restrict_matrix(z0, LANES, z1)
        multiply(b["T0"], g1, w, 0, x1, 8, y1, LANES)

        def finish(i, count):
            for q in range(count):
                for k in range(y1 // 8):
                    col = pltpu.roll(b["n"][pl.ds(8 * k, 8), :], turn(2 * LANES - (i + q)), 1)
                    v = g1[at(i + q, k, 0)] + jnp.where(lane8 == 0, col, 0.0)
                    g1[at(i + q, k, 0)] = v - mean_f

        groups(0, x1, 8, finish)
    moving = halo_send(1, HALO1, True)
    with jax.named_scope("pack1"):
        halo_pack(1, HALO1)
    moving = moving + halo_send(1, HALO1, False)
    wait(moving)
    with jax.named_scope("unpack1"):
        halo_unpack(1, HALO1)
    with jax.named_scope("first1"):
        ext_sweep("first", 1, g1, b1, 6)
    with jax.named_scope("defect1"):
        ext_sweep("defect", 1, b1, a1, 6)
    with jax.named_scope("restrict1"):
        e1 = ext[1]
        restrict_planes(a1, e1[0] - 1, y1 // 8, e1[1] // 8 - 1, e1[2], b["T1"], x2)
        w = restrict_matrix(2 * LANES, LANES, z2, 2 * LANES - 1)
        multiply(b["T1"], g2, w, 0, x2, x2, y2, LANES)
    moving = halo_send(2, HALO2, True)
    with jax.named_scope("pack2"):
        halo_pack(2, HALO2)
    moving = moving + halo_send(2, HALO2, False)
    wait(moving)
    with jax.named_scope("unpack2"):
        halo_unpack(2, HALO2)
    with jax.named_scope("sweeps2"):
        v, w2 = a2, b2
        ext_sweep("first", 2, g2, v, 9)
        for _ in range(COARSE_SWEEPS - 2):
            ext_sweep("relax", 2, v, w2, 9)
            v, w2 = w2, v
    with jax.named_scope("prolong1"):
        e2 = ext[2]
        q1, v1 = b["Q1"], b["V1"]
        w = prolong_matrix(LANES, 2 * LANES, z1, True)
        multiply(v, q1, w, 0, x2 + 2, (x2 + 2) // 3, e2[1], 2 * LANES)
        multiply(v, q1, w, e2[0] - 1, 1, 1, e2[1], 2 * LANES)
        nb2, top1 = e2[1] // 8, e1[1] // 8 - 1
        need = -(-(y1 + 3) // 16)

        def spread1(i, count):
            for q in range(count):
                for t in range(2):
                    for k in range(need):
                        spread_rows(q1, v1, i + q, k, k + 1, t, k)
                    spread_rows(q1, v1, i + q, nb2 - 1, 0, t, nb2 - 1)

        groups(0, x2 + 2, 3, spread1)
        spread1(e2[0] - 1, 1)

        def fine1(j, k, t):
            if k < top1:
                return v1[j, t, pl.ds(8 * k, 8), :]
            high = v1[j, t, pl.ds(8 * k, 8), :]
            low = v1[j, t, pl.ds(16 * nb2 - 8, 8), :]
            return jnp.where(row8 < 4, high, low)

        def add1(j, jn, i):
            for k in range(top1 + 1):
                for t in range(2):
                    c, n = fine1(j, k, t), fine1(jn, k, t)
                    b1[at(i, k, t)] = b1[at(i, k, t)] + c
                    b1[at(i + 1, k, t)] = b1[at(i + 1, k, t)] + 0.5 * (c + n)

        def add1_some(i, count):
            for q in range(count):
                add1(i + q, i + q + 1, 2 * (i + q))

        groups(0, x2 + 1, 2, add1_some)
        for k in range(top1 + 1):
            for t in range(2):
                b1[at(x1 + 2, k, t)] = b1[at(x1 + 2, k, t)] + fine1(x2 + 1, k, t)
        add1(e2[0] - 1, 0, e1[0] - 2)
    with jax.named_scope("post1"):
        ext_sweep("relax", 1, b1, a1, 6)
        ext_sweep("relax", 1, a1, b1, 6)
    with jax.named_scope("prolong0"):
        q0, v0 = b["Q0"], b["V0"]
        w = prolong_matrix(2 * LANES, z0, z0, False)
        multiply(b1, q0, w, 0, x1 + 1, 3, e1[1], z0)

        def spread0(i, count):
            for q in range(count):
                for t in range(nt0):
                    for k in range(y1 // 8):
                        spread_rows(q0, v0, i + q, k, k + 1, t, k)

        groups(0, x1 + 1, 3, spread0)
        shift = mean_u + 2.0 * W * mean_f

        def add0(j):
            for k in range(nb0):
                for t in range(nt0):
                    c = v0[j, t, pl.ds(8 * k, 8), :] - shift
                    n = v0[j + 1, t, pl.ds(8 * k, 8), :] - shift
                    b0[at(2 * j, k, t)] = b0[at(2 * j, k, t)] + c
                    b0[at(2 * j + 1, k, t)] = b0[at(2 * j + 1, k, t)] + 0.5 * (c + n)

        def add0_some(i, count):
            for q in range(count):
                add0(i + q)

        send_x, send_y, send_z = exchange(3, b0, b0.at[:, 0, :], b0.at[:, y0 - 1, :])
        add0(0)
        add0(x1 - 1)
        moving = send_x()
        groups(1, x1 - 1, 2, add0_some)
        moving = moving + send_y()

        def pack_b0(i, count):
            for q in range(count):
                pack_z(b["zp"].at[1], i + q, b0)

        groups(0, x0, 8, pack_b0)
        moving = moving + send_z()
    moving = sweep(3, moving, b0, a0, exchange(4, a0, *rows[4]), shift=W * mean_f)
    sweep(4, moving, a0, out, shift=W * mean_f)


def solution(mesh):
    counts = tuple(mesh.shape[a] for a in AXES)

    def shards(right_side, initial_guess):
        shape = right_side.shape
        dims = tuple(tuple(n >> l for n in shape) for l in range(3))
        cells = float(right_side.size)
        for n in counts:
            cells *= n
        bufs = buffers(dims, counts)
        messages = 5 * 6 + 7 + 2 * 26 + sum(counts) - 3
        return pl.pallas_call(
            functools.partial(kernel, dims, counts, tuple(bufs), cells),
            out_shape=jax.ShapeDtypeStruct(shape, jnp.float32),
            in_specs=[pl.BlockSpec(memory_space=pl.ANY)] * 2,
            out_specs=pl.BlockSpec(memory_space=pltpu.VMEM),
            scratch_shapes=list(bufs.values())
            + [pltpu.SemaphoreType.DMA((n,)) for n in (messages, messages, 2)],
            compiler_params=pltpu.CompilerParams(
                collective_id=0, has_side_effects=True, vmem_limit_bytes=56 * 1024 * 1024
            ),
        )(initial_guess, right_side)

    placed = (P(*AXES), P(*AXES))
    return jax.shard_map(
        shards, mesh=mesh, in_specs=placed, out_specs=P(*AXES), check_vma=False
    )
```

time: 196 us -> 86.8 us (0.44)
  Pallas kernels: 193 us -> 81.9 us
  local copies, waits for them, and re-layouts: 2.02 us -> 4.7 us
    pallas_call x1, Pallas kernels: 193 us -> 81.9 us  [shards(): pl.pallas_call(functools.partial(kernel, dims, counts, tuple(bufs), cells...]
    unnamed x1, local copies, waits for them, and re-layouts: 2.02 us -> 4.7 us
where the time goes in v1:
time: 86.8 us; the launch traced here: 86.6 us
  Pallas kernels  81.9 us (94%)
  local copies, waits for them, and re-layouts  4.7 us (5%)
    pallas_call x1, Pallas kernels, shards(): pl.pallas_call(functools.partial(kernel, dims, counts, tuple(bufs), cells...  81.9 us
    unnamed x1, local copies, waits for them, and re-layouts  4.7 us

profile of v1, /device:TPU:0, one launch (start us, length us, event | category | flops | bytes accessed | tf_op | source)
XLA Modules:
  0.0 86.6 jit_solution(14553887834972442289)
XLA Ops:
  0.0 81.9 %shard_map.28 = f32[64,64,256]{2,1,0:T(8,128)} custom-call(f32[64,64,256]{2,1,0:T(8,128)} %u_far.1, f32[64,64,256]{2,1,0:T(8,128)} %f_far.1), custom_call_target="tpu_custom_call" | custom-call | tf_op jit(solution)/shard_map/pallas_call | solution.py:772
  81.9 4.7 %copy.4 = f32[64,64,256]{2,1,0:T(8,128)} copy(f32[64,64,256]{2,1,0:T(8,128)} %shard_map.28) | data formatting | bytes 8388608

commit v2 on v1

v2 whole, which is shorter than its diff:
```python
import functools
import itertools

import jax
import jax.numpy as jnp
from jax import lax
from jax.experimental import pallas as pl
from jax.experimental.pallas import tpu as pltpu
from jax.sharding import PartitionSpec as P

COARSE_SWEEPS = 6
LANES = 128
AXES = ("gx", "gy", "gz")
relax_weight = 0.8
W = relax_weight / 6.0

SWEEP_PLANES = 10
FIX_PLANES = 12

HALO1 = (3, 4)
HALO2 = (COARSE_SWEEPS, COARSE_SWEEPS + 1)


def dot_split(a, w):
    hi = a.astype(jnp.bfloat16)
    mid = (a - hi.astype(jnp.float32)).astype(jnp.bfloat16)
    dot = functools.partial(jnp.dot, preferred_element_type=jnp.float32)
    return dot(hi, w) + dot(mid, w)


def iotas(shape):
    return (
        lax.broadcasted_iota(jnp.int32, shape, 0),
        lax.broadcasted_iota(jnp.int32, shape, 1),
    )


def restrict_matrix(rows, cols, count, wrap=None, step=1):
    r, c = iotas((rows, cols))
    d = jnp.abs(r - 2 * step * c)
    w = jnp.where(d == 0, 0.5, 0.0) + jnp.where(d == step, 0.25, 0.0)
    w = jnp.where((c < count) & (r < 2 * step * count), w, 0.0)
    if wrap is not None:
        w = w + jnp.where((r == wrap) & (c == 0), 0.25, 0.0)
    return w.astype(jnp.bfloat16)


def prolong_matrix(rows, cols, fine, wrapped):
    r, c = iotas((rows, cols))
    if wrapped:
        r = jnp.where(r < 3 * rows // 4, r, r - rows)
        c = jnp.where(c < 3 * cols // 4, c, c - cols)
    d = jnp.abs(c - 2 * r)
    w = jnp.where(d == 0, 1.0, 0.0) + jnp.where(d == 1, 0.5, 0.0)
    return w.astype(jnp.bfloat16)


def turn(by):
    return by % LANES if isinstance(by, int) else lax.rem(by, LANES)


OWN = 8


def extended(dims):
    (x1, y1, _), (x2, y2, _) = dims[1], dims[2]
    up = lambda n: -(-n // 8) * 8
    return (
        None,
        (x1 + sum(HALO1), up(y1 + OWN + HALO1[1] + 9), 2, HALO1[0]),
        (x2 + sum(HALO2), up(y2 + OWN + HALO2[1] + 4), 1, HALO2[0]),
    )


def buffers(dims, counts):
    (x, y, z), (x1, y1, _), (x2, y2, _) = dims
    ext = extended(dims)
    nt = z // LANES
    out = {}
    for name in ("u", "f", "A0", "B0"):
        out[name] = (x, nt, y + 2 * OWN, LANES)
    out["D0"] = (x + 1, nt, y + OWN, LANES)
    out["yp"] = (2, 2, nt, x, LANES)
    out["zp"] = (2, y, LANES)
    out["zh"] = (y, LANES)
    out["hx"] = (5, 2, nt, y, LANES)
    out["hy"] = (5, 2, nt, x, LANES)
    out["hz"] = (5, 2, y, LANES)
    out["rz"] = (y + OWN, LANES)
    out["rw"] = (y + OWN, LANES)
    out["m"] = (y + OWN, LANES)
    out["n"] = (y // 2, LANES)
    out["S"] = (4, nt, y + OWN, LANES)
    out["T0"] = (x1, nt, y1, LANES)
    out["T1"] = (x2, 2, y2, LANES)
    for l, ny in ((1, y1), (2, y2)):
        ex, ey, tiles, _ = ext[l]
        for name in "GAB":
            out[f"{name}{l}"] = (ex, tiles, ey, LANES)
        out[f"zp{l}"] = (2, ny, LANES)
        out[f"hz{l}"] = (2, 4, ey, LANES)
    out["P2"] = (x2 // 2 + -(-HALO2[0] // 2) + -(-HALO2[1] // 2), ext[2][1], LANES)
    out["Q1"] = (ext[2][0], 2, ext[2][1], LANES)
    out["V1"] = (ext[2][0], 2, ext[1][1] + 8, LANES)
    out["Q0"] = (x1 + 1, nt, ext[1][1], LANES)
    out["V0"] = (x1 + 1, nt, y, LANES)
    out["stats"] = (3, 2, 8, LANES)
    for a in range(3):
        out[f"sums{a}"] = (counts[a], 2, 8, LANES)
    return {k: pltpu.VMEM(v, jnp.float32) for k, v in out.items()}


def kernel(dims, counts, names, cells, u_far, f_far, out, *scratch):
    b = dict(zip(names, scratch[:-3]))
    send_sem, recv_sem, load_sem = scratch[-3:]
    u, f, a0, b0, d0 = b["u"], b["f"], b["A0"], b["B0"], b["D0"]
    loads = []
    for n, (far, near) in enumerate(((u_far, u), (f_far, f))):
        for t in range(2):
            lanes = pl.ds(LANES * t, LANES)
            own = near.at[:, t, pl.ds(OWN, dims[0][1]), :]
            c = pltpu.make_async_copy(far.at[:, :, lanes], own, load_sem.at[2 * n + t])
            c.start()
            loads.append(c)
    here = {a: lax.axis_index(a) for a in AXES}
    serial = itertools.count()
    ext = extended(dims)
    x0, y0, z0 = dims[0]
    x1, y1, z1 = dims[1]
    x2, y2, z2 = dims[2]
    nb0, nt0 = y0 // 8, z0 // LANES
    assert 2 * x0 == LANES and z1 == LANES and 2 * z2 == LANES
    assert nt0 == 2 and y2 % 8 == 0

    def device(offset):
        return tuple(lax.rem(here[a] + (o % n), n) for a, o, n in zip(AXES, offset, counts))

    def copy(src, dst, offset):
        k = next(serial)
        c = pltpu.make_async_remote_copy(
            src_ref=src,
            dst_ref=dst,
            send_sem=send_sem.at[k],
            recv_sem=recv_sem.at[k],
            device_id=device(offset),
            device_id_type=pl.DeviceIdType.MESH,
        )
        c.start()
        return c

    def wait(copies):
        with jax.named_scope("wait"):
            for c in copies:
                c.wait()

    around = [o for o in itertools.product((-1, 0, 1), repeat=3) if any(o)]
    offsets = list(around)
    for a in range(3):
        for j in range(2, counts[a] - 1):
            offsets.append(tuple(j if i == a else 0 for i in range(3)))
    barrier = pltpu.get_barrier_semaphore()
    for o in offsets:
        pl.semaphore_signal(
            barrier, inc=1, device_id=device(o), device_id_type=pl.DeviceIdType.MESH
        )

    row8 = lax.broadcasted_iota(jnp.int32, (8, LANES), 0)
    lane8 = lax.broadcasted_iota(jnp.int32, (8, LANES), 1)
    zero8 = jnp.zeros((8, LANES), jnp.float32)

    def at(i, k, t, first=OWN):
        return i, t, pl.ds(first + 8 * k, 8), slice(None)

    def groups(lo, hi, size, body):
        steps = (hi - lo) // size

        def step(p, _):
            body(lo + size * p, size)
            return 0

        if steps > 1:
            lax.fori_loop(0, steps, step, 0)
        elif steps:
            body(lo, size)
        if (hi - lo) % size:
            body(lo + size * steps, (hi - lo) % size)

    def lanes_of(rows):
        return lax.broadcasted_iota(jnp.int32, (rows, LANES), 1)

    def stencil(mode, l, src, g, i, near, first, rows, nt, z_wrap, shift=None):
        scale = 0.25**l
        lane = lanes_of(rows)
        here, above, below = (pl.ds(first + d, rows) for d in (0, -1, 1))
        c = [src[i, t, here, :] for t in range(nt)]
        left = [pltpu.roll(v, 1, 1) for v in c]
        right = [pltpu.roll(v, LANES - 1, 1) for v in c]
        new = []
        for t in range(nt):
            v = c[t]
            s = src[i, t, above, :] + src[i, t, below, :]
            for j in near:
                s = s + src[j, t, here, :]
            if z_wrap and nt == 1:
                s = s + (left[t] + right[t])
            else:
                before = left[t - 1] if t or z_wrap else 0.0
                after = right[(t + 1) % nt] if t < nt - 1 or z_wrap else 0.0
                z = jnp.where(lane == 0, before, left[t])
                s = s + (z + jnp.where(lane == LANES - 1, after, right[t]))
            if mode == "first":
                z = W / scale
                value = (W * z) * s + (W * (1.5 * z + 1.0 / scale)) * v
            elif mode == "defect":
                value = s - 6.0 * v
                value = g[i, t, here, :] + (value if l == 0 else scale * value)
            else:
                gv = g[i, t, here, :]
                value = s + 1.5 * v
                value = W * (value + (gv if l == 0 else (1.0 / scale) * gv))
                if shift is not None:
                    value = value - shift
            new.append(value)
        return new

    zh = b["zh"]
    last = LANES - 1

    def pack_z(zp, i, ref):
        lane = lanes_of(y0)
        both = jnp.where(lane == last, ref[i, nt0 - 1, own0, :], ref[i, 0, own0, :])
        moved = pltpu.roll(both, turn(2 * i + 1), 1)
        pltpu.store(zp, moved, mask=(lane == 2 * i) | (lane == 2 * i + 1))

    def pack_rows(yp, i, new):
        for side, r in ((0, 0), (1, y0 - 1)):
            for t in range(nt0):
                yp[side, t, pl.ds(i, 1), :] = new[t][r : r + 1]

    own0 = pl.ds(OWN, y0)

    def exchange(r, src, faces=None):
        hx, hy, hz = b["hx"].at[r], b["hy"].at[r], b["hz"].at[r]
        zp = b["zp"].at[r % 2]

        def send_x():
            return [
                copy(src.at[x0 - 1, :, own0], hx.at[0], (1, 0, 0)),
                copy(src.at[0, :, own0], hx.at[1], (-1, 0, 0)),
            ]

        def send_y():
            if faces is not None:
                return [
                    copy(faces.at[1], hy.at[0], (0, 1, 0)),
                    copy(faces.at[0], hy.at[1], (0, -1, 0)),
                ]
            started = []
            for t in range(nt0):
                started.append(copy(src.at[:, t, OWN + y0 - 1], hy.at[0, t], (0, 1, 0)))
                started.append(copy(src.at[:, t, OWN], hy.at[1, t], (0, -1, 0)))
            return started

        def send_z():
            return [
                copy(zp, hz.at[0], (0, 0, 1)),
                copy(zp, hz.at[1], (0, 0, -1)),
            ]

        return send_x, send_y, send_z

    def defect_exchange(r, d):
        rz, rw = b["rz"], b["rw"]
        yp, zp = b["yp"].at[r % 2], b["zp"].at[r % 2]

        def send_x():
            return [copy(d.at[x0 - 1, :, own0], d.at[x0, :, own0], (1, 0, 0))]

        def send_y():
            started = []
            for t in range(nt0):
                started.append(copy(yp.at[1, t, x0 - 1], d.at[x0, t, OWN - 1], (1, 1, 0)))
                started.append(copy(yp.at[1, t], d.at[pl.ds(0, x0), t, OWN - 1], (0, 1, 0)))
            return started

        def send_z():
            end, before = zp.at[pl.ds(y0 - 1, 1)], pl.ds(OWN - 1, 1)
            return [
                copy(end, rw.at[before], (1, 1, 1)),
                copy(zp, rw.at[own0], (1, 0, 1)),
                copy(end, rz.at[before], (0, 1, 1)),
                copy(zp, rz.at[own0], (0, 0, 1)),
            ]

        return send_x, send_y, send_z

    def sweep(r, moving, src, dst, onward=None, mode="relax", shift=None):
        hx, hy, hz = b["hx"].at[r], b["hy"].at[r], b["hz"].at[r]
        yp, zp = b["yp"].at[(r + 1) % 2], b["zp"].at[(r + 1) % 2]
        gain = 1.0 if mode == "defect" else W
        packed = onward is not None

        def plane(i, near):
            new = stencil(mode, 0, src, f, i, near, OWN, y0, nt0, False, shift)
            for t, value in enumerate(new):
                if packed:
                    dst[i, t, own0, :] = value
                else:
                    dst[i, :, pl.ds(LANES * t, LANES)] = value
            if packed:
                pack_rows(yp, i, new)

        def some(i, count):
            for q in range(count):
                plane(i + q, (i + q - 1, i + q + 1))
            if packed:
                for q in range(count):
                    pack_z(zp, i + q - 2, dst)

        with jax.named_scope("inner"):
            plane(0, (1,))
            plane(x0 - 1, (x0 - 2,))
            plane(1, (0, 2))
            plane(2, (1, 3))
            groups(3, x0 - 1, SWEEP_PLANES, some)
            if packed:
                pack_z(zp, x0 - 3, dst)
                pack_z(zp, x0 - 2, dst)
        wait(moving)
        odd = lane8 % 2 == 1
        for k in range(nb0):
            rows = pl.ds(8 * k, 8)
            before = pltpu.roll(hz[0, rows, :], 1, 1)
            after = pltpu.roll(hz[1, rows, :], LANES - 1, 1)
            zh[rows, :] = gain * jnp.where(odd, before, after)

        def fix(i, size, beyond=None):
            done = []
            lane = lanes_of(y0)
            for q in range(size):
                p = i + q
                halo = pltpu.roll(zh[...], turn(2 * LANES - 2 * p - 1), 1)
                for t in range(nt0):
                    where = (p, t) if packed else (p,)
                    start = OWN if packed else 0
                    cols = slice(None) if packed else pl.ds(LANES * t, LANES)
                    v = dst[where + (pl.ds(start, y0), cols)]
                    if beyond is not None:
                        v = v + gain * beyond[t]
                    if t == 0:
                        v = v + jnp.where(lane == 0, halo, 0.0)
                    if t == nt0 - 1:
                        v = v + jnp.where(lane == last, halo, 0.0)
                    low, high = (gain * hy[s, t, pl.ds(p, 1), :] for s in range(2))
                    low = v[:8] + jnp.where(row8 == 0, low, 0.0)
                    high = v[y0 - 8 :] + jnp.where(row8 == 7, high, 0.0)
                    done.append((where + (pl.ds(start, 8), cols), low))
                    done.append((where + (pl.ds(start + 8, y0 - 16), cols), v[8 : y0 - 8]))
                    done.append((where + (pl.ds(start + y0 - 8, 8), cols), high))
            for where, v in done:
                dst[where] = v

        with jax.named_scope("ends"):
            fix(0, 1, hx.at[0])
            fix(x0 - 1, 1, hx.at[1])
        if not packed:
            with jax.named_scope("fix"):
                groups(1, x0 - 1, FIX_PLANES, fix)
            return []
        started = onward[0]()
        with jax.named_scope("yface"):
            for side, r0 in ((0, 0), (1, y0 - 1)):
                line = jnp.broadcast_to(zh[pl.ds(r0, 1), :], (8, LANES))
                for j in range(x0 // 8):
                    slot = 2 * (8 * j + row8)
                    low = jnp.sum(jnp.where(lane8 == slot + 1, line, 0.0), 1, keepdims=True)
                    high = jnp.sum(jnp.where(lane8 == slot, line, 0.0), 1, keepdims=True)
                    for t in range(nt0):
                        rows = (side, t, pl.ds(8 * j, 8), slice(None))
                        v = yp[rows] + gain * hy[rows]
                        if t == 0:
                            v = v + jnp.where(lane8 == 0, low, 0.0)
                        if t == nt0 - 1:
                            v = v + jnp.where(lane8 == last, high, 0.0)
                        yp[rows] = v
                for i in (0, x0 - 1):
                    for t in range(nt0):
                        yp[side, t, pl.ds(i, 1), :] = dst[i, t, pl.ds(OWN + r0, 1), :]
        started = started + onward[1]()
        with jax.named_scope("zface"):
            for k in range(nb0):
                v = zp[pl.ds(8 * k, 8), :] + zh[pl.ds(8 * k, 8), :]
                for side, kk, rr in ((0, 0, 0), (1, nb0 - 1, 7)):
                    if k == kk:
                        total = zero8
                        for j in range(x0 // 8):
                            slot = 2 * (8 * j + row8)
                            low = hy[side, 0, pl.ds(8 * j, 8), :][:, :1]
                            high = hy[side, nt0 - 1, pl.ds(8 * j, 8), :][:, last:]
                            total = total + jnp.where(lane8 == slot + 1, low, 0.0)
                            total = total + jnp.where(lane8 == slot, high, 0.0)
                        total = gain * jnp.sum(total, 0, keepdims=True)
                        v = v + jnp.where(row8 == rr, total, 0.0)
                zp[pl.ds(8 * k, 8), :] = v
            pack_z(zp, 0, dst)
            pack_z(zp, x0 - 1, dst)
        started = started + onward[2]()
        with jax.named_scope("fix"):
            groups(1, x0 - 1, FIX_PLANES, fix)
        return started

    def restrict_xy(d, low, middle, j, u_slot, first, nb, nt, dst):
        s = b["S"].at[u_slot]
        n = dst.shape[2]
        rows = pl.ds(first, 8 * nb)
        for t in range(nt):
            v = 0.25 * (d[low, t, rows, :] + d[middle + 1, t, rows, :])
            s[t, rows, :] = v + 0.5 * d[middle, t, rows, :]
        for t in range(nt):
            around = s[t, pl.ds(OWN - 1, n, stride=2), :] + s[t, pl.ds(OWN + 1, n, stride=2), :]
            dst[j, t] = 0.25 * around + 0.5 * s[t, pl.ds(OWN, n, stride=2), :]

    def restrict_planes(d, before, origin, first, nb, nt, dst):
        restrict_xy(d, before, origin, 0, 0, first, nb, nt, dst)
        for j in range(1, 4):
            restrict_xy(d, origin + 2 * j - 1, origin + 2 * j, j, j, first, nb, nt, dst)

        def some(p, _):
            for q in range(4):
                j = 4 * p + q
                restrict_xy(d, origin + 2 * j - 1, origin + 2 * j, j, q, first, nb, nt, dst)
            return 0

        lax.fori_loop(1, dst.shape[0] // 4, some, 0)

    def planes_of(src, i, chunk, rows):
        parts = [src[pl.ds(i, chunk), t, rows, :] for t in range(src.shape[1])]
        parts = [v.reshape(chunk * v.shape[1], LANES) for v in parts]
        return jnp.concatenate(parts, 1) if len(parts) > 1 else parts[0]

    def multiply(src, dst, w, first, count, chunk, rows, shift, to_rows):
        tiles = w.shape[1] // LANES

        def step(k, _):
            i = first + k * chunk
            v = dot_split(planes_of(src, i, chunk, rows), w)
            for t in range(tiles):
                part = v[:, LANES * t : LANES * t + LANES]
                dst[pl.ds(i + shift, chunk), t, to_rows, :] = part.reshape(chunk, -1, LANES)
            return 0

        if count == chunk:
            step(0, 0)
        else:
            lax.fori_loop(0, count // chunk, step, 0)

    def region(o, start, n, depth):
        lo, hi = depth
        if o == 1:
            return pl.ds(start + n - lo, lo), pl.ds(start - lo, lo)
        if o == -1:
            return pl.ds(start, hi), pl.ds(start + n, hi)
        return pl.ds(start, n), pl.ds(start, n)

    def halo_send(l, g, nx, depth_x, depth, beside):
        zpl, hzl = b[f"zp{l}"], b[f"hz{l}"]
        ny = dims[l][1]
        started = []
        for o in sorted(around, key=lambda v: -sum(map(abs, v))):
            if (o[2] != 0) == beside:
                continue
            sx, dx = region(o[0], depth_x[0], nx, depth_x)
            sy, dy = region(o[1], OWN, ny, depth)
            if beside:
                started.append(copy(g.at[sx, sy], g.at[dx, dy], o))
            else:
                side = 0 if o[2] == 1 else 1
                half = {0: (0, 2), 1: (1, 1), -1: (0, 1)}[o[0]]
                slot = {0: 0, 1: 2, -1: 3}[o[0]]
                sy = pl.ds(sy.start - OWN, sy.size)
                source = zpl.at[pl.ds(*half), sy]
                started.append(copy(source, hzl.at[side, pl.ds(slot, half[1]), dy], o))
        return started

    def merge_sides(l, left):
        hzl = b[f"hz{l}"]
        for slot in range(4):
            for k in range(ext[l][1] // 8):
                rows = pl.ds(8 * k, 8)
                v = jnp.where(left, hzl[0, slot, rows, :], hzl[1, slot, rows, :])
                hzl[0, slot, rows, :] = v

    def halo_pack1():
        g, zpl = b["G1"], b["zp1"]
        lo, hi = HALO1
        width, per = lo + hi, x1 // 2
        for half in range(2):
            total = [zero8] * (y1 // 8)
            for p in range(per):
                first = width * p
                mask = (lane8 >= first) & (lane8 < first + width)
                for k in range(y1 // 8):
                    v = pltpu.roll(g[at(lo + half * per + p, k, 0)], first + lo, 1)
                    total[k] = jnp.where(mask, v, total[k])
            for k in range(y1 // 8):
                zpl[half, pl.ds(8 * k, 8), :] = total[k]

    def halo_unpack1():
        g, hzl = b["G1"], b["hz1"]
        lo, hi = HALO1
        width, per = lo + hi, x1 // 2
        left = lane8 < lo
        for p in range(1, per):
            left = left | ((lane8 >= width * p) & (lane8 < width * p + lo))
        merge_sides(1, left)
        for e in range(-lo, x1 + hi):
            if e < 0:
                slot, p = 2, e + per
            elif e < x1:
                slot, p = e // per, e % per
            else:
                slot, p = 3, e - x1
            back = LANES - (width * p + lo)
            for k in range(ext[1][1] // 8):
                v = hzl[0, slot, pl.ds(8 * k, 8), :]
                g[at(e + lo, k, 1, 0)] = pltpu.roll(v, back % LANES, 1)

    low_pairs, high_pairs = -(-HALO2[0] // 2), -(-HALO2[1] // 2)
    pairs, per2 = x2 // 2, x2 // 4
    assert sum(HALO2) <= 16 and per2 <= 4 and max(low_pairs, high_pairs) <= per2

    def halo_pack2():
        p2, zpl = b["P2"], b["zp2"]
        lo, hi = HALO2
        for half in range(2):
            total = [zero8] * (y2 // 8)
            for p in range(per2):
                first = lane8 % (LANES // 2) - 16 * p
                mask = (first >= 0) & (first < lo + hi)
                for k in range(y2 // 8):
                    v = p2[low_pairs + half * per2 + p, pl.ds(OWN + 8 * k, 8), :]
                    v = pltpu.roll(v, 16 * p + lo, 1)
                    total[k] = jnp.where(mask, v, total[k])
            for k in range(y2 // 8):
                zpl[half, pl.ds(8 * k, 8), :] = total[k]

    def halo_unpack2():
        g, p2, hzl = b["G2"], b["P2"], b["hz2"]
        lo, hi = HALO2
        half_lanes = LANES // 2
        for e in range(-lo, x2 + hi):
            pair, odd = (e + 2 * low_pairs) // 2, e % 2
            q = pair - low_pairs
            if q < 0:
                slot, p = 2, q + per2
            elif q < pairs:
                slot, p = q // per2, q % per2
            else:
                slot, p = 3, q - pairs
            back = LANES - (16 * p + lo) + (0 if odd else half_lanes)
            for k in range(ext[2][1] // 8):
                rows = pl.ds(8 * k, 8)
                own = p2[pair, rows, :]
                own = pltpu.roll(own, half_lanes, 1) if odd else own
                low = pltpu.roll(hzl[0, slot, rows, :], back % LANES, 1)
                high = pltpu.roll(hzl[1, slot, rows, :], back % LANES, 1)
                v = jnp.where(lane8 < 3 * half_lanes // 2, high, low)
                g[at(e + lo, k, 0, 0)] = jnp.where(lane8 < half_lanes, own, v)

    def ext_sweep(mode, l, src, dst, size, reach):
        nt, origin = ext[l][2], ext[l][3]
        nx, ny, _ = dims[l]
        g = b[f"G{l}"]
        first = OWN - reach[0]
        rows = 8 * -(-(ny + sum(reach)) // 8)

        def some(i, count):
            for q in range(count):
                p = i + q
                new = stencil(mode, l, src, g, p, (p - 1, p + 1), first, rows, nt, True)
                for t, value in enumerate(new):
                    dst[p, t, pl.ds(first, rows), :] = value

        groups(origin - reach[0], origin + nx + reach[1], size, some)

    def spread_rows(q, v, j, c0, t):
        c, n = q[at(j, 0, t, OWN + c0)], q[at(j, 0, t, OWN + c0 + 1)]
        return c, 0.5 * (c + n)

    st, sg = b["stats"], [b[f"sums{a}"] for a in range(3)]

    def spread_sums(a):
        return [
            copy(st.at[a], sg[a].at[j], tuple(j if i == a else 0 for i in range(3)))
            for j in range(1, counts[a])
        ]

    def gather_sums(a, copies):
        wait(copies)
        total = st[a]
        for j in range(1, counts[a]):
            total = total + sg[a][j]
        if a < 2:
            st[a + 1] = total
        return total

    def fold(ref):
        def step(p, totals):
            totals = list(totals)
            for q in range(2):
                for k in range(nb0):
                    for t in range(nt0):
                        totals[(2 * k + t) % 4] += ref[at(2 * p + q, k, t)]
            return tuple(totals)

        t = lax.fori_loop(0, x0 // 2, step, (zero8,) * 4)
        return (t[0] + t[1]) + (t[2] + t[3])

    a1, b1, g1 = b["A1"], b["B1"], b["G1"]
    a2, b2, g2 = b["A2"], b["B2"], b["G2"]

    with jax.named_scope("clear"):

        def clear0(i, _):
            for ref in (u, a0, b0):
                for t in range(nt0):
                    ref[i, t, pl.ds(0, OWN), :] = zero8
                    ref[i, t, pl.ds(OWN + y0, OWN), :] = zero8
            return 0

        lax.fori_loop(0, x0, clear0, 0)
        for l in (1, 2):
            ex, ey, tiles, _ = ext[l]
            refs = [b[f"{name}{l}"] for name in "GAB"]

            def clear(i, _, refs=refs, ey=ey, tiles=tiles):
                for ref in refs:
                    for k in range(ey // 8):
                        for t in range(tiles):
                            ref[at(i, k, t, 0)] = zero8
                return 0

            lax.fori_loop(0, ex, clear, 0)
            for side in range(2):
                for slot in range(4):
                    for k in range(ey // 8):
                        b[f"hz{l}"][side, slot, pl.ds(8 * k, 8), :] = zero8
        for p in range(b["P2"].shape[0]):
            for k in range(ext[2][1] // 8):
                b["P2"][p, pl.ds(8 * k, 8), :] = zero8
    with jax.named_scope("loadu"):
        loads[0].wait()
        loads[1].wait()
    with jax.named_scope("packu"):

        def pack_some(i, count):
            for q in range(count):
                pack_z(b["zp"].at[0], i + q, u)

        groups(0, x0, 8, pack_some)
    with jax.named_scope("sumu"):
        st[0, 0] = fold(u)
    with jax.named_scope("barrier"):
        pl.semaphore_wait(barrier, len(offsets))
    send_x, send_y, send_z = exchange(0, u)
    moving = send_x() + send_y() + send_z()
    with jax.named_scope("sumf"):
        loads[2].wait()
        loads[3].wait()
        st[0, 1] = fold(f)
    sums = spread_sums(0)
    faces = b["yp"]
    moving = sweep(0, moving, u, a0, exchange(1, a0, faces.at[1]))
    gather_sums(0, sums)
    sums = spread_sums(1)
    moving = sweep(1, moving, a0, b0, exchange(2, b0, faces.at[0]))
    gather_sums(1, sums)
    sums = spread_sums(2)
    moving = sweep(2, moving, b0, d0, defect_exchange(3, d0), mode="defect")
    total = gather_sums(2, sums)
    mean_u = jnp.sum(total[0]) * (1.0 / cells)
    mean_f = jnp.sum(total[1]) * (1.0 / cells)
    wait(moving)

    with jax.named_scope("restrict0"):
        lane = lax.broadcasted_iota(jnp.int32, (y0 + 8, LANES), 1)
        moved = pltpu.roll(b["rw"][...], 1, 1)
        rim = jnp.where(lane == last, moved, b["rz"][...])
        b["m"][...] = dot_split(rim, restrict_matrix(LANES, LANES, x1, last, 2))
        m = b["m"]
        v = 0.25 * (m[pl.ds(OWN - 1, y1, stride=2), :] + m[pl.ds(OWN + 1, y1, stride=2), :])
        b["n"][...] = 0.25 * (v + 0.5 * m[pl.ds(OWN, y1, stride=2), :])
        restrict_planes(d0, x0, 0, 0, nb0 + 1, nt0, b["T0"])
        w = restrict_matrix(z0, LANES, z1)
        o1, own1 = ext[1][3], pl.ds(OWN, y1)
        multiply(b["T0"], g1, w, 0, x1, 8, pl.ds(0, y1), o1, own1)

        def finish(i, count):
            for q in range(count):
                for k in range(y1 // 8):
                    col = pltpu.roll(b["n"][pl.ds(8 * k, 8), :], turn(2 * LANES - (i + q)), 1)
                    where = at(i + q + o1, k, 0)
                    g1[where] = g1[where] + jnp.where(lane8 == 0, col, 0.0) - mean_f

        groups(0, x1, 8, finish)
    moving = halo_send(1, g1.at[:, 0], x1, HALO1, HALO1, True)
    with jax.named_scope("pack1"):
        halo_pack1()
    moving = moving + halo_send(1, g1.at[:, 0], x1, HALO1, HALO1, False)
    wait(moving)
    with jax.named_scope("unpack1"):
        halo_unpack1()
    with jax.named_scope("first1"):
        ext_sweep("first", 1, g1, b1, 19, (2, 3))
    with jax.named_scope("defect1"):
        ext_sweep("defect", 1, b1, a1, 19, (1, 0))
    with jax.named_scope("restrict1"):
        t1 = b["T1"]
        blocks1 = -(-(y1 + 1) // 8)
        restrict_planes(a1, o1 - 1, o1, OWN - 1, blocks1, 2, t1)
        w = restrict_matrix(2 * LANES, LANES // 2, z2, 2 * LANES - 1)
        none = jnp.zeros_like(w)
        w = jnp.concatenate([jnp.concatenate([w, none], 1), jnp.concatenate([none, w], 1)], 0)
        paired = []
        for half in range(2):
            for t in range(2):
                v = [t1[2 * p + half, t] for p in range(pairs)]
                paired.append(jnp.concatenate(v, 0))
        v = dot_split(jnp.concatenate(paired, 1), w).reshape(pairs, y2, LANES)
        b["P2"][pl.ds(low_pairs, pairs), pl.ds(OWN, y2), :] = v
    depth2 = (low_pairs, high_pairs)
    moving = halo_send(2, b["P2"], pairs, depth2, HALO2, True)
    with jax.named_scope("pack2"):
        halo_pack2()
    moving = moving + halo_send(2, b["P2"], pairs, depth2, HALO2, False)
    wait(moving)
    with jax.named_scope("unpack2"):
        halo_unpack2()
    with jax.named_scope("sweeps2"):
        v, w2 = a2, b2
        reach = [(k + 1, k + 2) for k in range(COARSE_SWEEPS - 1)][::-1]
        ext_sweep("first", 2, g2, v, 27, reach[0])
        for k in range(1, COARSE_SWEEPS - 1):
            ext_sweep("relax", 2, v, w2, 27, reach[k])
            v, w2 = w2, v
    with jax.named_scope("prolong1"):
        o2 = ext[2][3]
        q1, v1 = b["Q1"], b["V1"]
        w = prolong_matrix(LANES, 2 * LANES, z1, True)
        multiply(v, q1, w, o2 - 1, x2 + 3, x2 + 3, pl.ds(0, ext[2][1]), 0, pl.ds(0, ext[2][1]))

        def spread1(i, count):
            for q in range(count):
                for t in range(2):
                    for c0 in range(-2, (y1 + 3) // 2, 8):
                        even, odd = spread_rows(q1, v1, i + q, c0, t)
                        v1[i + q, t, pl.ds(OWN + 2 * c0, 8, stride=2), :] = even
                        v1[i + q, t, pl.ds(OWN + 2 * c0 + 1, 8, stride=2), :] = odd

        groups(o2 - 1, o2 + x2 + 2, 5, spread1)

        def add1(i, count):
            for q in range(count):
                j = i + q
                for k in range(-(-(y1 + 5) // 8)):
                    for t in range(2):
                        c = v1[at(j + o2, k, t, OWN - 2)]
                        n = v1[at(j + 1 + o2, k, t, OWN - 2)]
                        even, odd = (at(2 * j + o1 + p, k, t, OWN - 2) for p in range(2))
                        b1[even] = b1[even] + c
                        b1[odd] = b1[odd] + 0.5 * (c + n)

        add1(-1, 1)
        groups(0, x2 + 1, 2, add1)
        for k in range(-(-(y1 + 5) // 8)):
            for t in range(2):
                even = at(x1 + 2 + o1, k, t, OWN - 2)
                b1[even] = b1[even] + v1[at(x2 + 1 + o2, k, t, OWN - 2)]
    with jax.named_scope("post1"):
        ext_sweep("relax", 1, b1, a1, 19, (1, 2))
        ext_sweep("relax", 1, a1, b1, 19, (0, 1))
    with jax.named_scope("prolong0"):
        q0, v0 = b["Q0"], b["V0"]
        w = prolong_matrix(2 * LANES, z0, z0, False)
        rows = pl.ds(OWN, y1 + 8)
        multiply(b1, q0, w, o1, x1 + 1, 3, rows, -o1, rows)

        def spread0(i, count):
            for q in range(count):
                for t in range(nt0):
                    for c0 in range(0, y1, 8):
                        even, odd = spread_rows(q0, v0, i + q, c0, t)
                        v0[i + q, t, pl.ds(2 * c0, 8, stride=2), :] = even
                        v0[i + q, t, pl.ds(2 * c0 + 1, 8, stride=2), :] = odd

        groups(0, x1 + 1, 3, spread0)
        shift = mean_u + 2.0 * W * mean_f

        def add0(i, count):
            for q in range(count):
                j = i + q
                for k in range(nb0):
                    for t in range(nt0):
                        c = v0[at(j, k, t, 0)] - shift
                        n = v0[at(j + 1, k, t, 0)] - shift
                        even, odd = at(2 * j, k, t), at(2 * j + 1, k, t)
                        b0[even] = b0[even] + c
                        b0[odd] = b0[odd] + 0.5 * (c + n)

        send_x, send_y, send_z = exchange(3, b0)
        add0(0, 1)
        add0(x1 - 1, 1)
        moving = send_x()
        groups(1, x1 - 1, 2, add0)
        moving = moving + send_y()

        def pack_b0(i, count):
            for q in range(count):
                pack_z(b["zp"].at[1], i + q, b0)

        groups(0, x0, 8, pack_b0)
        moving = moving + send_z()
    moving = sweep(3, moving, b0, a0, exchange(4, a0, faces.at[0]), shift=W * mean_f)
    sweep(4, moving, a0, out, shift=W * mean_f)


def solution(mesh):
    counts = tuple(mesh.shape[a] for a in AXES)

    def shards(right_side, initial_guess):
        shape = right_side.shape
        dims = tuple(tuple(n >> l for n in shape) for l in range(3))
        cells = float(right_side.size)
        for n in counts:
            cells *= n
        bufs = buffers(dims, counts)
        messages = 5 * 6 + 4 + 9 + 2 * 26 + sum(counts) - 3
        return pl.pallas_call(
            functools.partial(kernel, dims, counts, tuple(bufs), cells),
            out_shape=jax.ShapeDtypeStruct(shape, jnp.float32),
            in_specs=[pl.BlockSpec(memory_space=pl.ANY)] * 2,
            out_specs=pl.BlockSpec(memory_space=pltpu.VMEM),
            scratch_shapes=list(bufs.values())
            + [pltpu.SemaphoreType.DMA((n,)) for n in (messages, messages, 4)],
            compiler_params=pltpu.CompilerParams(
                collective_id=0, has_side_effects=True, vmem_limit_bytes=56 * 1024 * 1024
            ),
        )(initial_guess, right_side)

    placed = (P(*AXES), P(*AXES))
    return jax.shard_map(
        shards, mesh=mesh, in_specs=placed, out_specs=P(*AXES), check_vma=False
    )
```

time: 86.8 us -> 72 us (0.83)
  Pallas kernels: 81.9 us -> 67.2 us
    pallas_call x1, Pallas kernels: 81.9 us -> 67.2 us  [shards(): pl.pallas_call(functools.partial(kernel, dims, counts, tuple(bufs), cells...]
where the time goes in v2:
time: 72 us; the launch traced here: 71.9 us
  Pallas kernels  67.2 us (93%)
  local copies, waits for them, and re-layouts  4.7 us (7%)
    pallas_call x1, Pallas kernels, shards(): pl.pallas_call(functools.partial(kernel, dims, counts, tuple(bufs), cells...  67.2 us
    unnamed x1, local copies, waits for them, and re-layouts  4.7 us

profile of v2, /device:TPU:0, one launch (start us, length us, event | category | flops | bytes accessed | tf_op | source)
XLA Modules:
  0.0 71.9 jit_solution(6771007231878333027)
XLA Ops:
  0.0 67.2 %shard_map.28 = f32[64,64,256]{2,1,0:T(8,128)} custom-call(f32[64,64,256]{2,1,0:T(8,128)} %u_far.1, f32[64,64,256]{2,1,0:T(8,128)} %f_far.1), custom_call_target="tpu_custom_call" | custom-call | tf_op jit(solution)/shard_map/pallas_call | solution.py:838
  67.2 4.7 %copy.4 = f32[64,64,256]{2,1,0:T(8,128)} copy(f32[64,64,256]{2,1,0:T(8,128)} %shard_map.28) | data formatting | bytes 8388608

commit v3 on v2

--- a/solution.py
+++ b/solution.py
@@ -17,8 +17,8 @@
 SWEEP_PLANES = 10
 FIX_PLANES = 12
 
-HALO1 = (3, 4)
-HALO2 = (COARSE_SWEEPS, COARSE_SWEEPS + 1)
+HALO1 = (4, 5)
+HALO2 = (COARSE_SWEEPS + 1, COARSE_SWEEPS + 2)
 
 
 def dot_split(a, w):
@@ -53,6 +53,18 @@
     d = jnp.abs(c - 2 * r)
     w = jnp.where(d == 0, 1.0, 0.0) + jnp.where(d == 1, 0.5, 0.0)
     return w.astype(jnp.bfloat16)
+
+
+def hat_matrices(rows, cols):
+    r, c = iotas((rows, cols))
+    d = jnp.abs(c - 2 * jnp.where(r < 3 * rows // 4, r, r - rows))
+    parts = []
+    for row in ((1.0, 0.5), (1.0, 1.0, 0.5), (2.0, 1.5, 1.0, 0.5)):
+        w = jnp.zeros((rows, cols), jnp.float32)
+        for k, value in enumerate(row):
+            w = w + jnp.where(d == k, value, 0.0)
+        parts.append(w.astype(jnp.bfloat16))
+    return jnp.concatenate(parts, 1)
 
 
 def turn(by):
@@ -97,13 +109,14 @@
         ex, ey, tiles, _ = ext[l]
         for name in "GAB":
             out[f"{name}{l}"] = (ex, tiles, ey, LANES)
-        out[f"zp{l}"] = (2, ny, LANES)
-        out[f"hz{l}"] = (2, 4, ey, LANES)
+        packs = 2 if l == 2 else -(-x1 * sum(HALO1) // LANES)
+        out[f"zp{l}"] = (packs, ny, LANES)
+        out[f"hz{l}"] = (2, packs + 2, ey, LANES)
     out["P2"] = (x2 // 2 + -(-HALO2[0] // 2) + -(-HALO2[1] // 2), ext[2][1], LANES)
     out["Q1"] = (ext[2][0], 2, ext[2][1], LANES)
     out["V1"] = (ext[2][0], 2, ext[1][1] + 8, LANES)
-    out["Q0"] = (x1 + 1, nt, ext[1][1], LANES)
-    out["V0"] = (x1 + 1, nt, y, LANES)
+    for name in ("CA", "CB", "CC"):
+        out[name] = (x1 + 3, nt, ext[1][1], LANES)
     out["stats"] = (3, 2, 8, LANES)
     for a in range(3):
         out[f"sums{a}"] = (counts[a], 2, 8, LANES)
@@ -303,10 +316,7 @@
         def plane(i, near):
             new = stencil(mode, 0, src, f, i, near, OWN, y0, nt0, False, shift)
             for t, value in enumerate(new):
-                if packed:
-                    dst[i, t, own0, :] = value
-                else:
-                    dst[i, :, pl.ds(LANES * t, LANES)] = value
+                dst[i, t, own0, :] = value
             if packed:
                 pack_rows(yp, i, new)
 
@@ -341,10 +351,7 @@
                 p = i + q
                 halo = pltpu.roll(zh[...], turn(2 * LANES - 2 * p - 1), 1)
                 for t in range(nt0):
-                    where = (p, t) if packed else (p,)
-                    start = OWN if packed else 0
-                    cols = slice(None) if packed else pl.ds(LANES * t, LANES)
-                    v = dst[where + (pl.ds(start, y0), cols)]
+                    v = dst[p, t, own0, :]
                     if beyond is not None:
                         v = v + gain * beyond[t]
                     if t == 0:
@@ -354,11 +361,11 @@
                     low, high = (gain * hy[s, t, pl.ds(p, 1), :] for s in range(2))
                     low = v[:8] + jnp.where(row8 == 0, low, 0.0)
                     high = v[y0 - 8 :] + jnp.where(row8 == 7, high, 0.0)
-                    done.append((where + (pl.ds(start, 8), cols), low))
-                    done.append((where + (pl.ds(start + 8, y0 - 16), cols), v[8 : y0 - 8]))
-                    done.append((where + (pl.ds(start + y0 - 8, 8), cols), high))
-            for where, v in done:
-                dst[where] = v
+                    done.append((p, t, OWN, low))
+                    done.append((p, t, OWN + 8, v[8 : y0 - 8]))
+                    done.append((p, t, OWN + y0 - 8, high))
+            for p, t, start, v in done:
+                dst[p, t, pl.ds(start, v.shape[0]), :] = v
 
         with jax.named_scope("ends"):
             fix(0, 1, hx.at[0])
@@ -475,8 +482,9 @@
                 started.append(copy(g.at[sx, sy], g.at[dx, dy], o))
             else:
                 side = 0 if o[2] == 1 else 1
-                half = {0: (0, 2), 1: (1, 1), -1: (0, 1)}[o[0]]
-                slot = {0: 0, 1: 2, -1: 3}[o[0]]
+                packs = zpl.shape[0]
+                half = {0: (0, packs), 1: (packs - 1, 1), -1: (0, 1)}[o[0]]
+                slot = {0: 0, 1: packs, -1: packs + 1}[o[0]]
                 sy = pl.ds(sy.start - OWN, sy.size)
                 source = zpl.at[pl.ds(*half), sy]
                 started.append(copy(source, hzl.at[side, pl.ds(slot, half[1]), dy], o))
@@ -484,7 +492,7 @@
 
     def merge_sides(l, left):
         hzl = b[f"hz{l}"]
-        for slot in range(4):
+        for slot in range(hzl.shape[1]):
             for k in range(ext[l][1] // 8):
                 rows = pl.ds(8 * k, 8)
                 v = jnp.where(left, hzl[0, slot, rows, :], hzl[1, slot, rows, :])
@@ -493,10 +501,11 @@
     def halo_pack1():
         g, zpl = b["G1"], b["zp1"]
         lo, hi = HALO1
-        width, per = lo + hi, x1 // 2
-        for half in range(2):
+        width, packs = lo + hi, zpl.shape[0]
+        per = -(-x1 // packs)
+        for half in range(packs):
             total = [zero8] * (y1 // 8)
-            for p in range(per):
+            for p in range(min(per, x1 - half * per)):
                 first = width * p
                 mask = (lane8 >= first) & (lane8 < first + width)
                 for k in range(y1 // 8):
@@ -508,18 +517,20 @@
     def halo_unpack1():
         g, hzl = b["G1"], b["hz1"]
         lo, hi = HALO1
-        width, per = lo + hi, x1 // 2
+        width, packs = lo + hi, hzl.shape[1] - 2
+        per = -(-x1 // packs)
+        assert per * width <= LANES and hi <= per and lo <= x1 - (packs - 1) * per
         left = lane8 < lo
         for p in range(1, per):
             left = left | ((lane8 >= width * p) & (lane8 < width * p + lo))
         merge_sides(1, left)
         for e in range(-lo, x1 + hi):
             if e < 0:
-                slot, p = 2, e + per
+                slot, p = packs, x1 + e - (packs - 1) * per
             elif e < x1:
                 slot, p = e // per, e % per
             else:
-                slot, p = 3, e - x1
+                slot, p = packs + 1, e - x1
             back = LANES - (width * p + lo)
             for k in range(ext[1][1] // 8):
                 v = hzl[0, slot, pl.ds(8 * k, 8), :]
@@ -642,7 +653,7 @@
 
             lax.fori_loop(0, ex, clear, 0)
             for side in range(2):
-                for slot in range(4):
+                for slot in range(b[f"hz{l}"].shape[1]):
                     for k in range(ey // 8):
                         b[f"hz{l}"][side, slot, pl.ds(8 * k, 8), :] = zero8
         for p in range(b["P2"].shape[0]):
@@ -677,6 +688,18 @@
     gather_sums(1, sums)
     sums = spread_sums(2)
     moving = sweep(2, moving, b0, d0, defect_exchange(3, d0), mode="defect")
+    with jax.named_scope("step3"):
+
+        def step3(i, count):
+            for q in range(count):
+                for t in range(nt0):
+                    a0[i + q, t, own0, :] = b0[i + q, t, own0, :] + W * d0[i + q, t, own0, :]
+            for q in range(count):
+                pack_z(b["zp"].at[0], i + q, a0)
+
+        groups(0, x0, 8, step3)
+    send_x, send_y, send_z = exchange(4, a0)
+    moving3 = send_x() + send_y() + send_z()
     total = gather_sums(2, sums)
     mean_u = jnp.sum(total[0]) * (1.0 / cells)
     mean_f = jnp.sum(total[1]) * (1.0 / cells)
@@ -707,11 +730,12 @@
     with jax.named_scope("pack1"):
         halo_pack1()
     moving = moving + halo_send(1, g1.at[:, 0], x1, HALO1, HALO1, False)
+    sweep(4, moving3, a0, b0)
     wait(moving)
     with jax.named_scope("unpack1"):
         halo_unpack1()
     with jax.named_scope("first1"):
-        ext_sweep("first", 1, g1, b1, 19, (2, 3))
+        ext_sweep("first", 1, g1, b1, 13, (3, 4))
     with jax.named_scope("defect1"):
         ext_sweep("defect", 1, b1, a1, 19, (1, 0))
     with jax.named_scope("restrict1"):
@@ -738,7 +762,7 @@
         halo_unpack2()
     with jax.named_scope("sweeps2"):
         v, w2 = a2, b2
-        reach = [(k + 1, k + 2) for k in range(COARSE_SWEEPS - 1)][::-1]
+        reach = [(k + 2, k + 3) for k in range(COARSE_SWEEPS - 1)][::-1]
         ext_sweep("first", 2, g2, v, 27, reach[0])
         for k in range(1, COARSE_SWEEPS - 1):
             ext_sweep("relax", 2, v, w2, 27, reach[k])
@@ -747,7 +771,7 @@
         o2 = ext[2][3]
         q1, v1 = b["Q1"], b["V1"]
         w = prolong_matrix(LANES, 2 * LANES, z1, True)
-        multiply(v, q1, w, o2 - 1, x2 + 3, x2 + 3, pl.ds(0, ext[2][1]), 0, pl.ds(0, ext[2][1]))
+        multiply(v, q1, w, o2 - 2, x2 + 5, x2 + 5, pl.ds(0, ext[2][1]), 0, pl.ds(0, ext[2][1]))
 
         def spread1(i, count):
             for q in range(count):
@@ -757,71 +781,82 @@
                         v1[i + q, t, pl.ds(OWN + 2 * c0, 8, stride=2), :] = even
                         v1[i + q, t, pl.ds(OWN + 2 * c0 + 1, 8, stride=2), :] = odd
 
-        groups(o2 - 1, o2 + x2 + 2, 5, spread1)
+        groups(o2 - 2, o2 + x2 + 3, 7, spread1)
 
         def add1(i, count):
             for q in range(count):
                 j = i + q
-                for k in range(-(-(y1 + 5) // 8)):
-                    for t in range(2):
-                        c = v1[at(j + o2, k, t, OWN - 2)]
-                        n = v1[at(j + 1 + o2, k, t, OWN - 2)]
-                        even, odd = (at(2 * j + o1 + p, k, t, OWN - 2) for p in range(2))
-                        b1[even] = b1[even] + c
-                        b1[odd] = b1[odd] + 0.5 * (c + n)
-
-        add1(-1, 1)
-        groups(0, x2 + 1, 2, add1)
-        for k in range(-(-(y1 + 5) // 8)):
-            for t in range(2):
-                even = at(x1 + 2 + o1, k, t, OWN - 2)
-                b1[even] = b1[even] + v1[at(x2 + 1 + o2, k, t, OWN - 2)]
+                rows = pl.ds(OWN - 3, 8 * -(-(y1 + 7) // 8))
+                for t in range(2):
+                    c, n = v1[j + o2, t, rows, :], v1[j + 1 + o2, t, rows, :]
+                    even, odd = 2 * j + o1, 2 * j + o1 + 1
+                    b1[even, t, rows, :] = b1[even, t, rows, :] + c
+                    b1[odd, t, rows, :] = b1[odd, t, rows, :] + 0.5 * (c + n)
+
+        groups(-2, x2 + 2, 4, add1)
     with jax.named_scope("post1"):
-        ext_sweep("relax", 1, b1, a1, 19, (1, 2))
-        ext_sweep("relax", 1, a1, b1, 19, (0, 1))
-    with jax.named_scope("prolong0"):
-        q0, v0 = b["Q0"], b["V0"]
-        w = prolong_matrix(2 * LANES, z0, z0, False)
-        rows = pl.ds(OWN, y1 + 8)
-        multiply(b1, q0, w, o1, x1 + 1, 3, rows, -o1, rows)
-
-        def spread0(i, count):
+        ext_sweep("relax", 1, b1, a1, 19, (2, 3))
+        ext_sweep("relax", 1, a1, b1, 18, (1, 2))
+    keep = 1.0 - relax_weight
+    coarse = [b[name] for name in ("CA", "CB", "CC")]
+    fine = [u, d0, a0]
+
+    def spread(a, bb, c):
+        be, bo = bb[-1] + bb[1], bb[0] + bb[1]
+        ce, co = c[0] + c[0] + (c[-1] + c[1]), c[0] + c[1]
+        e0 = a[0] + (bb[0] + 0.5 * be) + ce
+        o0 = 0.5 * ((a[0] + a[1]) + (c[-1] + c[2])) + (bo + 1.5 * co)
+        return e0, o0, (bb[0] + ce, 0.5 * bo + 2.0 * co), (c[0], 0.5 * co)
+
+    with jax.named_scope("tailz"):
+        shift = mean_u + 4.0 * W * mean_f
+        w = hat_matrices(2 * LANES, z0)
+        chunk, rows = 5, pl.ds(OWN - 1, y1 + 8)
+
+        def tail_z(k, _):
+            i = k * chunk
+            v = dot_split(planes_of(b1, i + o1 - 1, chunk, rows), w)
+            for t in range(nt0):
+                z = [v[:, z0 * n + LANES * t : z0 * n + LANES * t + LANES] for n in range(3)]
+                ca = keep**2 * z[0] + (2.0 * keep * W) * z[1] + W**2 * z[2] - shift
+                cb = (2.0 * keep * W) * z[0] + (2.0 * W**2) * z[1]
+                for ref, value in zip(coarse, (ca, cb, W**2 * z[0])):
+                    ref[pl.ds(i, chunk), t, rows, :] = value.reshape(chunk, -1, LANES)
+            return 0
+
+        assert (x1 + 3) % chunk == 0
+        lax.fori_loop(0, (x1 + 3) // chunk, tail_z, 0)
+    with jax.named_scope("taily"):
+
+        def tail_y(i, count):
             for q in range(count):
                 for t in range(nt0):
-                    for c0 in range(0, y1, 8):
-                        even, odd = spread_rows(q0, v0, i + q, c0, t)
-                        v0[i + q, t, pl.ds(2 * c0, 8, stride=2), :] = even
-                        v0[i + q, t, pl.ds(2 * c0 + 1, 8, stride=2), :] = odd
-
-        groups(0, x1 + 1, 3, spread0)
-        shift = mean_u + 2.0 * W * mean_f
-
-        def add0(i, count):
+                    near = [
+                        {d: ref[i + q, t, pl.ds(OWN + d, y1), :] for d in (-1, 0, 1, 2)}
+                        for ref in coarse
+                    ]
+                    e0, o0, one, two = spread(*near)
+                    for ref, even, odd in ((fine[0], e0, o0), (fine[1], *one), (fine[2], *two)):
+                        ref[i + q, t, pl.ds(0, y1, stride=2), :] = even
+                        ref[i + q, t, pl.ds(1, y1, stride=2), :] = odd
+
+        groups(0, x1 + 3, 5, tail_y)
+    with jax.named_scope("tailx"):
+        rows0 = pl.ds(0, y0)
+
+        def tail_x(i, count):
             for q in range(count):
                 j = i + q
-                for k in range(nb0):
-                    for t in range(nt0):
-                        c = v0[at(j, k, t, 0)] - shift
-                        n = v0[at(j + 1, k, t, 0)] - shift
-                        even, odd = at(2 * j, k, t), at(2 * j + 1, k, t)
-                        b0[even] = b0[even] + c
-                        b0[odd] = b0[odd] + 0.5 * (c + n)
-
-        send_x, send_y, send_z = exchange(3, b0)
-        add0(0, 1)
-        add0(x1 - 1, 1)
-        moving = send_x()
-        groups(1, x1 - 1, 2, add0)
-        moving = moving + send_y()
-
-        def pack_b0(i, count):
-            for q in range(count):
-                pack_z(b["zp"].at[1], i + q, b0)
-
-        groups(0, x0, 8, pack_b0)
-        moving = moving + send_z()
-    moving = sweep(3, moving, b0, a0, exchange(4, a0, faces.at[0]), shift=W * mean_f)
-    sweep(4, moving, a0, out, shift=W * mean_f)
+                for t in range(nt0):
+                    near = [
+                        {d: ref[j + 1 + d, t, rows0, :] for d in (-1, 0, 1, 2)} for ref in fine
+                    ]
+                    e0, o0, _, _ = spread(*near)
+                    lanes = pl.ds(LANES * t, LANES)
+                    out[2 * j, :, lanes] = b0[2 * j, t, own0, :] + e0
+                    out[2 * j + 1, :, lanes] = b0[2 * j + 1, t, own0, :] + o0
+
+        groups(0, x1, 4, tail_x)
 
 
 def solution(mesh):
@@ -834,7 +869,7 @@
         for n in counts:
             cells *= n
         bufs = buffers(dims, counts)
-        messages = 5 * 6 + 4 + 9 + 2 * 26 + sum(counts) - 3
+        messages = 2 * 8 + 2 * 6 + 9 + 2 * 26 + sum(counts) - 3
         return pl.pallas_call(
             functools.partial(kernel, dims, counts, tuple(bufs), cells),
             out_shape=jax.ShapeDtypeStruct(shape, jnp.float32),

time: 72 us -> 65.7 us (0.913)
  Pallas kernels: 67.2 us -> 60.8 us
    pallas_call x1, Pallas kernels: 67.2 us -> 60.8 us  [shards(): pl.pallas_call(functools.partial(kernel, dims, counts, tuple(bufs), cells...]
where the time goes in v3:
time: 65.7 us; the launch traced here: 65.5 us
  Pallas kernels  60.8 us (93%)
  local copies, waits for them, and re-layouts  4.7 us (7%)
    pallas_call x1, Pallas kernels, shards(): pl.pallas_call(functools.partial(kernel, dims, counts, tuple(bufs), cells...  60.8 us
    unnamed x1, local copies, waits for them, and re-layouts  4.7 us

profile of v3, /device:TPU:0, one launch (start us, length us, event | category | flops | bytes accessed | tf_op | source)
XLA Modules:
  0.0 65.5 jit_solution(12848981147322045813)
XLA Ops:
  0.0 60.8 %shard_map.28 = f32[64,64,256]{2,1,0:T(8,128)} custom-call(f32[64,64,256]{2,1,0:T(8,128)} %u_far.1, f32[64,64,256]{2,1,0:T(8,128)} %f_far.1), custom_call_target="tpu_custom_call" | custom-call | tf_op jit(solution)/shard_map/pallas_call | solution.py:873
  60.8 4.7 %copy.4 = f32[64,64,256]{2,1,0:T(8,128)} copy(f32[64,64,256]{2,1,0:T(8,128)} %shard_map.28) | data formatting | bytes 8388608

commit v4 on v3

--- a/solution.py
+++ b/solution.py
@@ -24,8 +24,9 @@
 def dot_split(a, w):
     hi = a.astype(jnp.bfloat16)
     mid = (a - hi.astype(jnp.float32)).astype(jnp.bfloat16)
-    dot = functools.partial(jnp.dot, preferred_element_type=jnp.float32)
-    return dot(hi, w) + dot(mid, w)
+    rows = a.shape[0]
+    v = jnp.dot(jnp.concatenate([hi, mid], 0), w, preferred_element_type=jnp.float32)
+    return v[:rows] + v[rows:]
 
 
 def iotas(shape):
@@ -91,7 +92,10 @@
     out = {}
     for name in ("u", "f", "A0", "B0"):
         out[name] = (x, nt, y + 2 * OWN, LANES)
-    out["D0"] = (x + 1, nt, y + OWN, LANES)
+    out["D0"] = (x, nt, y + OWN, LANES)
+    out["rx"] = (nt, y + OWN, LANES)
+    out["ry"] = (nt, x + OWN, LANES)
+    out["e"] = (x1 + y1, LANES)
     out["yp"] = (2, 2, nt, x, LANES)
     out["zp"] = (2, y, LANES)
     out["zh"] = (y, LANES)
@@ -287,13 +291,14 @@
         yp, zp = b["yp"].at[r % 2], b["zp"].at[r % 2]
 
         def send_x():
-            return [copy(d.at[x0 - 1, :, own0], d.at[x0, :, own0], (1, 0, 0))]
+            return [copy(d.at[x0 - 1, :, own0], b["rx"].at[:, own0], (1, 0, 0))]
 
         def send_y():
             started = []
             for t in range(nt0):
-                started.append(copy(yp.at[1, t, x0 - 1], d.at[x0, t, OWN - 1], (1, 1, 0)))
-                started.append(copy(yp.at[1, t], d.at[pl.ds(0, x0), t, OWN - 1], (0, 1, 0)))
+                ry = b["ry"].at[t]
+                started.append(copy(yp.at[1, t, x0 - 1], ry.at[OWN - 1], (1, 1, 0)))
+                started.append(copy(yp.at[1, t], ry.at[pl.ds(OWN, x0)], (0, 1, 0)))
             return started
 
         def send_z():
@@ -336,7 +341,7 @@
             if packed:
                 pack_z(zp, x0 - 3, dst)
                 pack_z(zp, x0 - 2, dst)
-        wait(moving)
+        wait(moving() if callable(moving) else moving)
         odd = lane8 % 2 == 1
         for k in range(nb0):
             rows = pl.ds(8 * k, 8)
@@ -421,7 +426,8 @@
         n = dst.shape[2]
         rows = pl.ds(first, 8 * nb)
         for t in range(nt):
-            v = 0.25 * (d[low, t, rows, :] + d[middle + 1, t, rows, :])
+            v = d[middle + 1, t, rows, :]
+            v = 0.25 * (v if low is None else v + d[low, t, rows, :])
             s[t, rows, :] = v + 0.5 * d[middle, t, rows, :]
         for t in range(nt):
             around = s[t, pl.ds(OWN - 1, n, stride=2), :] + s[t, pl.ds(OWN + 1, n, stride=2), :]
@@ -445,12 +451,14 @@
         parts = [v.reshape(chunk * v.shape[1], LANES) for v in parts]
         return jnp.concatenate(parts, 1) if len(parts) > 1 else parts[0]
 
-    def multiply(src, dst, w, first, count, chunk, rows, shift, to_rows):
+    def multiply(src, dst, w, first, count, chunk, rows, shift, to_rows, less=None):
         tiles = w.shape[1] // LANES
 
         def step(k, _):
             i = first + k * chunk
             v = dot_split(planes_of(src, i, chunk, rows), w)
+            if less is not None:
+                v = v - less
             for t in range(tiles):
                 part = v[:, LANES * t : LANES * t + LANES]
                 dst[pl.ds(i + shift, chunk), t, to_rows, :] = part.reshape(chunk, -1, LANES)
@@ -469,16 +477,14 @@
             return pl.ds(start, hi), pl.ds(start + n, hi)
         return pl.ds(start, n), pl.ds(start, n)
 
-    def halo_send(l, g, nx, depth_x, depth, beside):
+    def halo_send(l, g, nx, depth_x, depth):
         zpl, hzl = b[f"zp{l}"], b[f"hz{l}"]
         ny = dims[l][1]
         started = []
         for o in sorted(around, key=lambda v: -sum(map(abs, v))):
-            if (o[2] != 0) == beside:
-                continue
             sx, dx = region(o[0], depth_x[0], nx, depth_x)
             sy, dy = region(o[1], OWN, ny, depth)
-            if beside:
+            if o[2] == 0:
                 started.append(copy(g.at[sx, sy], g.at[dx, dy], o))
             else:
                 side = 0 if o[2] == 1 else 1
@@ -633,11 +639,15 @@
     with jax.named_scope("clear"):
 
         def clear0(i, _):
-            for ref in (u, a0, b0):
+            for ref in (u, a0, b0, d0):
                 for t in range(nt0):
                     ref[i, t, pl.ds(0, OWN), :] = zero8
-                    ref[i, t, pl.ds(OWN + y0, OWN), :] = zero8
+                    if ref is not d0:
+                        ref[i, t, pl.ds(OWN + y0, OWN), :] = zero8
             return 0
+
+        for t in range(nt0):
+            b["rx"][t, pl.ds(0, OWN), :] = zero8
 
         lax.fori_loop(0, x0, clear0, 0)
         for l in (1, 2):
@@ -688,6 +698,15 @@
     gather_sums(1, sums)
     sums = spread_sums(2)
     moving = sweep(2, moving, b0, d0, defect_exchange(3, d0), mode="defect")
+    total = gather_sums(2, sums)
+    mean_u = jnp.sum(total[0]) * (1.0 / cells)
+    mean_f = jnp.sum(total[1]) * (1.0 / cells)
+
+    o1, own1 = ext[1][3], pl.ds(OWN, y1)
+    w0 = restrict_matrix(z0, LANES, z1)
+    with jax.named_scope("restrict0"):
+        restrict_planes(d0, None, 0, 0, nb0 + 1, nt0, b["T0"])
+        multiply(b["T0"], g1, w0, 0, x1, 8, pl.ds(0, y1), o1, own1, mean_f)
     with jax.named_scope("step3"):
 
         def step3(i, count):
@@ -698,66 +717,77 @@
                 pack_z(b["zp"].at[0], i + q, a0)
 
         groups(0, x0, 8, step3)
-    send_x, send_y, send_z = exchange(4, a0)
-    moving3 = send_x() + send_y() + send_z()
-    total = gather_sums(2, sums)
-    mean_u = jnp.sum(total[0]) * (1.0 / cells)
-    mean_f = jnp.sum(total[1]) * (1.0 / cells)
     wait(moving)
 
-    with jax.named_scope("restrict0"):
+    with jax.named_scope("edges0"):
         lane = lax.broadcasted_iota(jnp.int32, (y0 + 8, LANES), 1)
         moved = pltpu.roll(b["rw"][...], 1, 1)
         rim = jnp.where(lane == last, moved, b["rz"][...])
         b["m"][...] = dot_split(rim, restrict_matrix(LANES, LANES, x1, last, 2))
-        m = b["m"]
-        v = 0.25 * (m[pl.ds(OWN - 1, y1, stride=2), :] + m[pl.ds(OWN + 1, y1, stride=2), :])
-        b["n"][...] = 0.25 * (v + 0.5 * m[pl.ds(OWN, y1, stride=2), :])
-        restrict_planes(d0, x0, 0, 0, nb0 + 1, nt0, b["T0"])
-        w = restrict_matrix(z0, LANES, z1)
-        o1, own1 = ext[1][3], pl.ds(OWN, y1)
-        multiply(b["T0"], g1, w, 0, x1, 8, pl.ds(0, y1), o1, own1)
+        m, edge = b["m"], b["e"]
+
+        def every_other(ref, n):
+            v = 0.25 * (ref[pl.ds(OWN - 1, n, stride=2), :] + ref[pl.ds(OWN + 1, n, stride=2), :])
+            return 0.25 * (v + 0.5 * ref[pl.ds(OWN, n, stride=2), :])
+
+        rims = []
+        for t in range(nt0):
+            ry, rx = every_other(b["ry"].at[t], x1), every_other(b["rx"].at[t], y1)
+            rims.append(jnp.concatenate([ry, rx], 0))
+        edge[...] = dot_split(jnp.concatenate(rims, 1), w0)
+        b["n"][...] = every_other(m, y1)
+        g1[o1, 0, own1, :] = g1[o1, 0, own1, :] + edge[pl.ds(x1, y1), :]
 
         def finish(i, count):
+            lane = lanes_of(y1)
+            done = []
             for q in range(count):
-                for k in range(y1 // 8):
-                    col = pltpu.roll(b["n"][pl.ds(8 * k, 8), :], turn(2 * LANES - (i + q)), 1)
-                    where = at(i + q + o1, k, 0)
-                    g1[where] = g1[where] + jnp.where(lane8 == 0, col, 0.0) - mean_f
-
-        groups(0, x1, 8, finish)
-    moving = halo_send(1, g1.at[:, 0], x1, HALO1, HALO1, True)
+                col = pltpu.roll(b["n"][...], turn(2 * LANES - (i + q)), 1)
+                v = g1[i + q + o1, 0, own1, :] + jnp.where(lane == 0, col, 0.0)
+                top = v[:8] + jnp.where(row8 == 0, edge[pl.ds(i + q, 1), :], 0.0)
+                done.append((i + q + o1, OWN, top))
+                done.append((i + q + o1, OWN + 8, v[8:]))
+            for p, start, v in done:
+                g1[p, 0, pl.ds(start, v.shape[0]), :] = v
+
+        groups(0, x1, 16, finish)
     with jax.named_scope("pack1"):
         halo_pack1()
-    moving = moving + halo_send(1, g1.at[:, 0], x1, HALO1, HALO1, False)
-    sweep(4, moving3, a0, b0)
-    wait(moving)
-    with jax.named_scope("unpack1"):
-        halo_unpack1()
-    with jax.named_scope("first1"):
-        ext_sweep("first", 1, g1, b1, 13, (3, 4))
-    with jax.named_scope("defect1"):
-        ext_sweep("defect", 1, b1, a1, 19, (1, 0))
-    with jax.named_scope("restrict1"):
-        t1 = b["T1"]
-        blocks1 = -(-(y1 + 1) // 8)
-        restrict_planes(a1, o1 - 1, o1, OWN - 1, blocks1, 2, t1)
-        w = restrict_matrix(2 * LANES, LANES // 2, z2, 2 * LANES - 1)
-        none = jnp.zeros_like(w)
-        w = jnp.concatenate([jnp.concatenate([w, none], 1), jnp.concatenate([none, w], 1)], 0)
-        paired = []
-        for half in range(2):
-            for t in range(2):
-                v = [t1[2 * p + half, t] for p in range(pairs)]
-                paired.append(jnp.concatenate(v, 0))
-        v = dot_split(jnp.concatenate(paired, 1), w).reshape(pairs, y2, LANES)
-        b["P2"][pl.ds(low_pairs, pairs), pl.ds(OWN, y2), :] = v
+    moving = halo_send(1, g1.at[:, 0], x1, HALO1, HALO1)
+    t1 = b["T1"]
     depth2 = (low_pairs, high_pairs)
-    moving = halo_send(2, b["P2"], pairs, depth2, HALO2, True)
-    with jax.named_scope("pack2"):
-        halo_pack2()
-    moving = moving + halo_send(2, b["P2"], pairs, depth2, HALO2, False)
-    wait(moving)
+    halo2 = []
+
+    def between():
+        wait(moving)
+        send_x, send_y, send_z = exchange(4, a0)
+        started = send_x() + send_y() + send_z()
+        with jax.named_scope("unpack1"):
+            halo_unpack1()
+        with jax.named_scope("first1"):
+            ext_sweep("first", 1, g1, b1, 13, (3, 4))
+        with jax.named_scope("defect1"):
+            ext_sweep("defect", 1, b1, a1, 19, (1, 0))
+        with jax.named_scope("restrict1"):
+            blocks1 = -(-(y1 + 1) // 8)
+            restrict_planes(a1, o1 - 1, o1, OWN - 1, blocks1, 2, t1)
+            w = restrict_matrix(2 * LANES, LANES // 2, z2, 2 * LANES - 1)
+            none = jnp.zeros_like(w)
+            w = jnp.concatenate([jnp.concatenate([w, none], 1), jnp.concatenate([none, w], 1)], 0)
+            paired = []
+            for half in range(2):
+                for t in range(2):
+                    v = [t1[2 * p + half, t] for p in range(pairs)]
+                    paired.append(jnp.concatenate(v, 0))
+            v = dot_split(jnp.concatenate(paired, 1), w).reshape(pairs, y2, LANES)
+            b["P2"][pl.ds(low_pairs, pairs), pl.ds(OWN, y2), :] = v
+        with jax.named_scope("pack2"):
+            halo_pack2()
+        halo2.extend(halo_send(2, b["P2"], pairs, depth2, HALO2))
+        return started
+
+    sweep(4, between, a0, b0)
+    wait(halo2)
     with jax.named_scope("unpack2"):
         halo_unpack2()
     with jax.named_scope("sweeps2"):
@@ -811,7 +841,7 @@
     with jax.named_scope("tailz"):
         shift = mean_u + 4.0 * W * mean_f
         w = hat_matrices(2 * LANES, z0)
-        chunk, rows = 5, pl.ds(OWN - 1, y1 + 8)
+        chunk, rows = x1 + 3, pl.ds(OWN - 1, y1 + 8)
 
         def tail_z(k, _):
             i = k * chunk
@@ -824,8 +854,7 @@
                     ref[pl.ds(i, chunk), t, rows, :] = value.reshape(chunk, -1, LANES)
             return 0
 
-        assert (x1 + 3) % chunk == 0
-        lax.fori_loop(0, (x1 + 3) // chunk, tail_z, 0)
+        tail_z(0, 0)
     with jax.named_scope("taily"):
 
         def tail_y(i, count):

time: 65.7 us -> 60.9 us (0.927)
  Pallas kernels: 60.8 us -> 56 us
    pallas_call x1, Pallas kernels: 60.8 us -> 56 us  [shards(): pl.pallas_call(functools.partial(kernel, dims, counts, tuple(bufs), cells...]
where the time goes in v4:
time: 60.9 us; the launch traced here: 60.7 us
  Pallas kernels  56 us (92%)
  local copies, waits for them, and re-layouts  4.7 us (8%)
    pallas_call x1, Pallas kernels, shards(): pl.pallas_call(functools.partial(kernel, dims, counts, tuple(bufs), cells...  56 us
    unnamed x1, local copies, waits for them, and re-layouts  4.7 us

profile of v4, /device:TPU:0, one launch (start us, length us, event | category | flops | bytes accessed | tf_op | source)
XLA Modules:
  0.0 60.7 jit_solution(869566164229189149)
XLA Ops:
  0.0 56.0 %shard_map.28 = f32[64,64,256]{2,1,0:T(8,128)} custom-call(f32[64,64,256]{2,1,0:T(8,128)} %u_far.1, f32[64,64,256]{2,1,0:T(8,128)} %f_far.1), custom_call_target="tpu_custom_call" | custom-call | tf_op jit(solution)/shard_map/pallas_call | solution.py:902
  56.0 4.7 %copy.4 = f32[64,64,256]{2,1,0:T(8,128)} copy(f32[64,64,256]{2,1,0:T(8,128)} %shard_map.28) | data formatting | bytes 8388608
